TPU v7x, 32 devices: a 4x2x2 block of a 4x4x8 slice. The times are simulated.
32 devices in a mesh: dp: 4 (over y, z), tp: 8 (over x, core).
Axes of the slice: x: 4, y: 2, z: 2, core: 2. Of those that a mesh axis runs over, the one named last changes fastest.
The devices are a block of a 4x4x8 slice.
Arguments:
- tokens: bfloat16 [4, 2048, 2048], P('dp', 'tp'), parts along dimension 0
- doc_ids: int32 [4, 2048], P('dp', 'tp'), parts along dimension 0
- norm1_gain: float32 [2, 2048], replicated
- norm1_shift: float32 [2, 2048], replicated
- qkv_weight: bfloat16 [2, 2048, 3, 32, 64], P(None, None, None, 'tp')
- out_weight: bfloat16 [2, 32, 64, 2048], P(None, 'tp')
- out_bias: float32 [2, 2048], replicated
- norm2_gain: float32 [2, 2048], replicated
- norm2_shift: float32 [2, 2048], replicated
- up_weight: bfloat16 [2, 2048, 8192], P(None, None, 'tp')
- up_bias: float32 [2, 8192], P(None, 'tp')
- down_weight: bfloat16 [2, 8192, 2048], P(None, 'tp')
- down_bias: float32 [2, 2048], replicated
Outputs:
- output: bfloat16 [4, 2048, 2048], P('dp', 'tp'), parts along dimension 0
There are 4 independent parts. A program takes and returns all parts, laid end to end along the dimension named above; an argument that names none is the same for every part.
All inputs are finite; a program needn't handle non-finite values.
Results may differ from a plain program's by a relative error of at most 0.0119882.
Values are sent between devices in bfloat16 or wider.
A program may use at most 768 MiB of HBM per device.

v0:
```python
import jax
import jax.numpy as jnp
from jax import lax
from jax.sharding import PartitionSpec as P, NamedSharding

QUERY_ROWS = 512


def layer_norm(residual, gain_vec, shift_vec):
    mean_val = jnp.mean(residual, axis=-1, keepdims=True)
    centered = residual - mean_val
    variance = jnp.mean(centered * centered, axis=-1, keepdims=True)
    return (centered * lax.rsqrt(variance + 1e-5) * gain_vec + shift_vec).astype(jnp.bfloat16)


def doc_causal_attention(queries, keys_in, values_in, all_ids):
    seq_len = queries.shape[2]
    score_scale = queries.shape[3] ** -0.5
    block_rows = min(QUERY_ROWS, seq_len)
    pieces = []
    for start_row in range(0, seq_len, block_rows):
        stop_row = start_row + block_rows
        scores = jnp.einsum("bhqe,bhke->bhqk", queries[:, :, start_row:stop_row], keys_in[:, :, :stop_row], preferred_element_type=jnp.float32) * score_scale
        query_pos = start_row + jnp.arange(block_rows)
        key_pos = jnp.arange(stop_row)
        allowed = (key_pos[None, None, :] <= query_pos[None, :, None]) & (all_ids[:, start_row:stop_row, None] == all_ids[:, None, :stop_row])
        scores = jnp.where(allowed[:, None], scores, -1e30)
        probs_blk = jax.nn.softmax(scores, axis=-1).astype(jnp.bfloat16)
        pieces.append(jnp.einsum("bhqk,bhke->bqhe", probs_blk, values_in[:, :, :stop_row], preferred_element_type=jnp.float32).astype(jnp.bfloat16))
    return jnp.concatenate(pieces, axis=1)


def scatter_sum(partial_rows, groups):
    n_batch, seq_len, model_dim = partial_rows.shape
    split_rows = partial_rows.reshape(n_batch, groups, seq_len // groups, model_dim)
    received = lax.all_to_all(split_rows, "tp", 1, 1, tiled=True)
    return jnp.sum(received, axis=1, dtype=jnp.float32)


def solution(mesh):
    groups = mesh.shape["tp"]
    row_spec = P("dp", "tp", None)
    vec_spec = P(None, None)
    in_specs = (row_spec, P("dp", "tp"), vec_spec, vec_spec, P(None, None, None, "tp", None), P(None, "tp", None, None), vec_spec, vec_spec, vec_spec, P(None, None, "tp"), P(None, "tp"), P(None, "tp", None), vec_spec)

    def device_fn(tokens, doc_ids, norm1_gain, norm1_shift, qkv_weight, out_weight, out_bias, norm2_gain, norm2_shift, up_weight, up_bias, down_weight, down_bias):
        all_ids = lax.all_gather(doc_ids, "tp", axis=1, tiled=True)
        residual = tokens.astype(jnp.float32)
        for layer_idx in range(norm1_gain.shape[0]):
            normed = layer_norm(residual, norm1_gain[layer_idx], norm1_shift[layer_idx])
            full_rows = lax.all_gather(normed, "tp", axis=1, tiled=True)
            qkv_heads = jnp.einsum("bsd,dthe->tbhse", full_rows, qkv_weight[layer_idx], preferred_element_type=jnp.float32).astype(jnp.bfloat16)
            attn_out = doc_causal_attention(qkv_heads[0], qkv_heads[1], qkv_heads[2], all_ids)
            attn_part = jnp.einsum("bshe,hed->bsd", attn_out, out_weight[layer_idx], preferred_element_type=jnp.float32).astype(jnp.bfloat16)
            residual = residual + (scatter_sum(attn_part, groups) + out_bias[layer_idx])
            normed2 = layer_norm(residual, norm2_gain[layer_idx], norm2_shift[layer_idx])
            full_rows2 = lax.all_gather(normed2, "tp", axis=1, tiled=True)
            pre_act = jnp.einsum("bsd,df->bsf", full_rows2, up_weight[layer_idx], preferred_element_type=jnp.float32) + up_bias[layer_idx]
            hidden = jax.nn.gelu(pre_act, approximate=True).astype(jnp.bfloat16)
            mlp_part = jnp.einsum("bsf,fd->bsd", hidden, down_weight[layer_idx], preferred_element_type=jnp.float32).astype(jnp.bfloat16)
            residual = residual + (scatter_sum(mlp_part, groups) + down_bias[layer_idx])
        return residual.astype(jnp.bfloat16)

    return jax.shard_map(device_fn, mesh=mesh, in_specs=in_specs, out_specs=row_spec, check_vma=False)
```

profile of v0, /device:TPU:81, one launch (start us, length us, event | category | flops | bytes accessed | tf_op | source)
XLA Modules:
  0.0 846.7 jit_solution(6166908463376159880)
XLA Ops:
  9.4 1.4 convert_reduce_fusion.4
  10.8 1.6 fusion.100
  12.5 2.8 fusion.103
  15.3 12.3 %all_gather.18 = s32[1,2048]{1,0:T(1,128)S(1)} all-gather(s32[1,256]{1,0:T(1,128)S(1)} %copy-done.21), channel_id=1, replica_groups=mesh['dp'=4,'tp'=8] {'tp'}, dimensions={1}, use_global_device_ids=true | all-gather | bytes 9216 | tf_op jit(solution)/shard_map/all_gather | solution.py:47
  29.2 2.0 fusion.90
  31.2 1.7 fusion.97
  32.8 5.4 fusion.225
  38.2 28.2 %all-gather.5.cloned.1.call-done = bf16[1,2048,2048]{2,1,0:T(8,128)(2,1)} async-done(((bf16[1,256,2048]{2,1,0:T(8,128)(2,1)}), bf16[1,2048,2048]{2,1,0:T(8,128)(2,1)}) %all-gather.5.cloned.1.call-update) | async-done | bytes 8388624 | tf_op jit(solution)/shard_map/all_gather | solution.py:51
  66.4 9.1 %fusion.34 = f32[2048,768]{0,1:S(1)} fusion(bf16[2048,768]{0,1:T(8,128)(2,1)S(1)} %bitcast.354, bf16[1,2048,2048]{2,1,0:T(8,128)(2,1)} %all-gather.5.cloned.1.call-done), kind=kOutput, calls=%fused_computation.54 | convolution fusion | flops 6442450944 | bytes 17825792
  76.0 1.8 slice_bitcast_fusion.3
  77.8 11.1 %fusion.234 = (f32[4,512]{1,0:T(4,128)S(1)}, f32[4,512,2048]{2,1,0:T(8,128)}) fusion(pred[512,2048]{1,0:T(8,128)(4,1)} %fusion.90, bf16[3,1,4,2048,64]{3,4,2,0,1:T(8,128)(2,1)S(1)} %convert_bitcast_fusion.1, bf16[1,4,2048,64]{2,3,1,0:T(8,128)(2,1)} %get-tuple-element.16), kind=kOutput, calls=%fused_computation.293 | convolution fusion | flops 553650176 | bytes 19144704 | tf_op jit(solution)/shard_map/sub | solution.py:28
  88.9 7.6 fusion.185
  96.5 7.6 fusion.240
  104.1 4.7 fusion.241
  108.7 8.6 %fusion.131 = bf16[1,512,4,64]{1,3,2,0:T(8,128)(2,1)S(1)} fusion(f32[4,512,2048]{2,1,0:T(8,128)} %get-tuple-element.36, f32[4,512]{1,0:T(4,128)S(1)} %get-tuple-element.35, bf16[3,1,4,2048,64]{3,4,2,0,1:T(8,128)(2,1)S(1)} %convert_bitcast_fusion.1), kind=kOutput, calls=%fused_computation.167 | convolution fusion | flops 545390592 | bytes 18096128 | tf_op jit(solution)/shard_map/bhqk,bhke->bqhe/dot_general | solution.py:29
  117.3 16.2 %fusion.239 = (f32[4,512]{1,0:T(4,128)S(1)}, f32[4,512,1536]{2,1,0:T(8,128)}) fusion(f32[4,512,1536]{2,1,0:T(8,128)} %fusion.185, pred[512,1536]{1,0:T(8,128)(4,1)S(1)} %copy-done.6), kind=kOutput, calls=%fused_computation.294 | output fusion | flops 18875904 | bytes 25960448 | tf_op jit(solution)/shard_map/sub | solution.py:28
  133.6 6.7 fusion.129
  140.3 5.0 fusion.133
  146.9 5.6 bitcast_convert_fusion.1
  152.5 5.3 all-to-all-start
  159.6 91.7 %all-to-all-done = bf16[1,8,256,2048]{3,2,0,1:T(8,128)(2,1)} async-done(((bf16[1,8,256,2048]{3,2,0,1:T(8,128)(2,1)}), bf16[1,8,256,2048]{3,2,0,1:T(8,128)(2,1)}, u32[]{:S(2)}, u32[]{:S(2)}) %all-to-all-start) | async-done | bytes 8388640 | tf_op jit(solution)/shard_map/all_to_all | solution.py:36
  251.3 5.3 convert_reduce_fusion.3
  257.6 1.6 add_convert_fusion.2
  259.9 46.1 %all-gather.7.cloned.1.call-done = bf16[1,2048,2048]{2,1,0:T(8,128)(2,1)} async-done(((bf16[1,256,2048]{2,1,0:T(8,128)(2,1)}), bf16[1,2048,2048]{2,1,0:T(8,128)(2,1)}) %all-gather.7.cloned.1.call-update) | async-done | bytes 8388624 | tf_op jit(solution)/shard_map/all_gather | solution.py:57
  306.0 25.7 %convolution_convert_fusion.1 = bf16[2048,2048]{1,0:T(8,128)(2,1)} fusion(bf16[1,2048,2048]{2,1,0:T(8,128)(2,1)} %all-gather.7.cloned.1.call-done, bf16[2,1024,2048]{2,1,0:T(8,128)(2,1)} %param.24, f32[1024]{0:T(1024)S(1)} %bitcast.377, bf16[2,2048,1024]{2,1,0:T(8,128)(2,1)} %param.22), kind=kOutput, calls=%fused_computation.71 | convolution fusion | flops 17205035008 | bytes 25169920 | tf_op jit(solution)/shard_map/bsf,fd->bsd/dot_general | solution.py:60
  331.7 5.2 all-to-all-start.1
  337.6 93.0 %all-to-all-done.1 = bf16[1,8,256,2048]{3,2,0,1:T(8,128)(2,1)} async-done(((bf16[1,8,256,2048]{3,2,0,1:T(8,128)(2,1)}), bf16[1,8,256,2048]{3,2,0,1:T(8,128)(2,1)}, u32[]{:S(2)}, u32[]{:S(2)}) %all-to-all-start.1) | async-done | bytes 8388640 | tf_op jit(solution)/shard_map/all_to_all | solution.py:36
  430.6 5.4 convert_reduce_fusion.2
  438.0 1.4 add_convert_fusion.1
  439.6 46.7 %all-gather.9.cloned.1.call-done = bf16[1,2048,2048]{2,1,0:T(8,128)(2,1)} async-done(((bf16[1,256,2048]{2,1,0:T(8,128)(2,1)}), bf16[1,2048,2048]{2,1,0:T(8,128)(2,1)}) %all-gather.9.cloned.1.call-update) | async-done | bytes 8388624 | tf_op jit(solution)/shard_map/all_gather | solution.py:51
  486.2 9.2 %fusion.30 = f32[2048,768]{0,1:S(1)} fusion(bf16[2048,768]{0,1:T(8,128)(2,1)S(1)} %bitcast.353, bf16[1,2048,2048]{2,1,0:T(8,128)(2,1)} %all-gather.9.cloned.1.call-done), kind=kOutput, calls=%fused_computation.50 | convolution fusion | flops 6442450944 | bytes 17825792
  496.0 1.7 slice_bitcast_fusion.2
  497.7 10.6 %fusion.242 = (f32[4,512]{1,0:T(4,128)S(1)}, f32[4,512,2048]{2,1,0:T(8,128)}) fusion(pred[512,2048]{1,0:T(8,128)(4,1)} %fusion.90, bf16[3,1,4,2048,64]{3,4,2,0,1:T(8,128)(2,1)S(1)} %convert_bitcast_fusion, bf16[1,4,2048,64]{2,3,1,0:T(8,128)(2,1)} %get-tuple-element.13), kind=kOutput, calls=%fused_computation.297 | convolution fusion | flops 553650176 | bytes 19144704 | tf_op jit(solution)/shard_map/sub | solution.py:28
  508.3 7.6 fusion.184
  516.0 7.5 fusion.248
  523.4 4.8 fusion.249
  528.2 16.5 %fusion.247 = (f32[4,512]{1,0:T(4,128)S(1)}, f32[4,512,1536]{2,1,0:T(8,128)}) fusion(f32[4,512,1536]{2,1,0:T(8,128)} %fusion.184, pred[512,1536]{1,0:T(8,128)(4,1)} %fusion.97), kind=kOutput, calls=%fused_computation.298 | output fusion | flops 18875904 | bytes 25960448 | tf_op jit(solution)/shard_map/sub | solution.py:28
  544.7 8.6 %fusion.132 = bf16[1,512,4,64]{1,3,2,0:T(8,128)(2,1)S(1)} fusion(f32[4,512,2048]{2,1,0:T(8,128)} %get-tuple-element.44, f32[4,512]{1,0:T(4,128)S(1)} %get-tuple-element.43, bf16[3,1,4,2048,64]{3,4,2,0,1:T(8,128)(2,1)S(1)} %convert_bitcast_fusion), kind=kOutput, calls=%fused_computation.168 | convolution fusion | flops 545390592 | bytes 18096128 | tf_op jit(solution)/shard_map/bhqk,bhke->bqhe/dot_general | solution.py:29
  554.4 2.4 fusion.130
  556.8 5.0 fusion.134
  563.4 2.4 bitcast_convert_fusion
  565.8 97.2 %all_to_all.20 = bf16[1,8,256,2048]{3,2,0,1:T(8,128)(2,1)S(1)} all-to-all(bf16[1,8,256,2048]{3,2,0,1:T(8,128)(2,1)S(1)} %bitcast.349), channel_id=1, replica_groups=mesh['dp'=4,'tp'=8] {'tp'}, dimensions={1} | all-to-all | bytes 16777216 | tf_op jit(solution)/shard_map/all_to_all | solution.py:36
  663.0 1.8 convert_reduce_fusion.1
  665.5 1.4 add_convert_fusion
  667.0 46.8 %all-gather.11.cloned.1.call-done = bf16[1,2048,2048]{2,1,0:T(8,128)(2,1)} async-done(((bf16[1,256,2048]{2,1,0:T(8,128)(2,1)}), bf16[1,2048,2048]{2,1,0:T(8,128)(2,1)}) %all-gather.11.cloned.1.call-update) | async-done | bytes 8388624 | tf_op jit(solution)/shard_map/all_gather | solution.py:57
  713.8 25.3 %convolution_convert_fusion = bf16[2048,2048]{1,0:T(8,128)(2,1)} fusion(bf16[1,2048,2048]{2,1,0:T(8,128)(2,1)} %all-gather.11.cloned.1.call-done, bf16[2,1024,2048]{2,1,0:T(8,128)(2,1)} %param.24, f32[1024]{0:T(1024)S(1)} %bitcast.376, bf16[2,2048,1024]{2,1,0:T(8,128)(2,1)} %param.22), kind=kOutput, calls=%fused_computation.70 | convolution fusion | flops 17205035008 | bytes 25169920 | tf_op jit(solution)/shard_map/bsf,fd->bsd/dot_general | solution.py:60
  739.2 97.5 %all_to_all.21 = bf16[1,8,256,2048]{3,2,0,1:T(8,128)(2,1)S(1)} all-to-all(bf16[1,8,256,2048]{3,2,0,1:T(8,128)(2,1)} %bitcast.350), channel_id=1, replica_groups=mesh['dp'=4,'tp'=8] {'tp'}, dimensions={1} | all-to-all | bytes 16777216 | tf_op jit(solution)/shard_map/all_to_all | solution.py:36
  836.7 1.8 convert_reduce_fusion
  (96 shorter events, 17.8 us)
Async XLA Ops:
  6.5 8.7 %copy-start.21 = (s32[1,256]{1,0:T(1,128)S(1)}, s32[1,256]{1,0:T(1,128)}, u32[]{:S(2)}) copy-start(s32[1,256]{1,0:T(1,128)} %param.14) | copy-start | bytes 3076
  6.5 59.8 %all-gather.5.cloned.1.call-start = ((), (), s32[]{:S(2)}) async-start(), calls=%async_computation.4 | async-start | bytes 9437184 | tf_op jit(solution)/shard_map/all_gather | solution.py:51
  27.9 76.2 %copy-start.7 = (pred[512,512]{0,1:T(8,128)(4,1)}, pred[512,512]{0,1:T(8,128)(4,1)S(1)}, u32[]{:S(2)}) copy-start(pred[512,512]{0,1:T(8,128)(4,1)S(1)} %fusion.169) | copy-start | bytes 786436
  108.7 8.6 %copy-start.6 = (pred[512,1536]{1,0:T(8,128)(4,1)S(1)}, pred[512,1536]{1,0:T(8,128)(4,1)}, u32[]{:S(2)}) copy-start(pred[512,1536]{1,0:T(8,128)(4,1)} %fusion.97) | copy-start | bytes 2359300
  117.3 16.3 %copy-start.5 = (bf16[1,4,2048,64]{2,3,1,0:T(8,128)(2,1)S(1)}, bf16[1,4,2048,64]{2,3,1,0:T(8,128)(2,1)}, u32[]{:S(2)}) copy-start(bf16[1,4,2048,64]{2,3,1,0:T(8,128)(2,1)} %get-tuple-element.14) | copy-start | bytes 3145732
  140.3 5.0 copy-start.26
  145.3 1.6 copy-start.22
  152.5 5.3 copy-start.15
  152.5 5.9 copy-start.16
  152.5 6.5 copy-start.17
  152.5 98.9 %all-to-all-start = ((bf16[1,8,256,2048]{3,2,0,1:T(8,128)(2,1)}), bf16[1,8,256,2048]{3,2,0,1:T(8,128)(2,1)}, u32[]{:S(2)}, u32[]{:S(2)}) async-start(bf16[1,8,256,2048]{3,2,0,1:T(8,128)(2,1)} %bitcast.347), calls=%async_computation | async-start | bytes 16777216 | tf_op jit(solution)/shard_map/all_to_all | solution.py:36
  157.7 148.3 %all-gather.7.cloned.1.call-start = ((), (), s32[]{:S(2)}) async-start(), calls=%async_computation.5 | async-start | bytes 9437184 | tf_op jit(solution)/shard_map/all_gather | solution.py:57
  159.6 97.1 %copy-start = (bf16[1,256,2048]{2,1,0:T(8,128)(2,1)S(1)}, bf16[1,256,2048]{2,1,0:T(8,128)(2,1)}, u32[]{:S(2)}) copy-start(bf16[1,256,2048]{2,1,0:T(8,128)(2,1)} %param.13) | copy-start | bytes 3145732
  257.0 2.2 copy-start.19
  331.7 5.3 copy-start.18
  331.7 98.8 %all-to-all-start.1 = ((bf16[1,8,256,2048]{3,2,0,1:T(8,128)(2,1)}), bf16[1,8,256,2048]{3,2,0,1:T(8,128)(2,1)}, u32[]{:S(2)}, u32[]{:S(2)}) async-start(bf16[1,8,256,2048]{3,2,0,1:T(8,128)(2,1)} %bitcast.348), calls=%async_computation.1 | async-start | bytes 16777216 | tf_op jit(solution)/shard_map/all_to_all | solution.py:36
  336.9 149.3 %all-gather.9.cloned.1.call-start = ((), (), s32[]{:S(2)}) async-start(), calls=%async_computation.6 | async-start | bytes 9437184 | tf_op jit(solution)/shard_map/all_gather | solution.py:51
  436.0 2.1 copy-start.9
  436.0 2.0 copy-start.10
  436.7 1.3 copy-start.1
  436.7 49.5 %copy-start.3 = (bf16[1,2048,3,4,64]{1,4,3,2,0:T(8,128)(2,1)S(1)}, bf16[1,2048,3,4,64]{1,4,3,2,0:T(8,128)(2,1)}, u32[]{:S(2)}) copy-start(bf16[1,2048,3,4,64]{1,4,3,2,0:T(8,128)(2,1)} %get-tuple-element.9) | copy-start | bytes 9437188
  439.5 274.3 %all-gather.11.cloned.1.call-start = ((), (), s32[]{:S(2)}) async-start(), calls=%async_computation.7 | async-start | bytes 9437184 | tf_op jit(solution)/shard_map/all_gather | solution.py:57
  516.0 7.5 copy-start.8
  544.7 8.7 %copy-start.4 = (bf16[1,4,2048,64]{2,3,1,0:T(8,128)(2,1)S(1)}, bf16[1,4,2048,64]{2,3,1,0:T(8,128)(2,1)}, u32[]{:S(2)}) copy-start(bf16[1,4,2048,64]{2,3,1,0:T(8,128)(2,1)} %get-tuple-element.11) | copy-start | bytes 3145732
  544.7 9.7 %copy-start.24 = (f32[4,512,1536]{2,1,0:T(8,128)S(1)}, f32[4,512,1536]{2,1,0:T(8,128)}, u32[]{:S(2)}) copy-start(f32[4,512,1536]{2,1,0:T(8,128)} %get-tuple-element.46) | copy-start | bytes 37748740
  556.8 5.0 copy-start.25
  561.8 1.6 copy-start.23
  663.0 1.8 copy-start.2
  663.0 1.8 copy-start.13
  664.8 0.7 copy-start.11
  664.8 0.7 copy-start.12
  665.1 48.7 %copy-start.20 = (f32[1,1024]{1,0:T(1,128)S(1)}, f32[1,1024]{1,0:T(1,128)}, u32[]{:S(2)}) copy-start(f32[1,1024]{1,0:T(1,128)} %get-tuple-element.29) | copy-start | bytes 12292
  836.7 1.8 copy-start.14
Sparse Core Ops, SparseCore 0:
  15.4 50.9 all-gather.4
  259.4 46.5 all-gather.6
  439.6 46.5 all-gather.8
  667.1 46.6 all-gather.10
where the time goes:
time: 856 us; the launch traced here: 847 us
  waiting for transfers between devices  353 us (41%)
  blocking collectives  207 us (24%)
  matrix products  176 us (21%)
  other arithmetic  67.5 us (8%)
  local copies, waits for them, and re-layouts  18.9 us (2%)
  between operations  14 us (2%)
  starting transfers between devices  10.6 us (1%)
    all_to_all x2, blocking collectives, scatter_sum(): received = lax.all_to_all(split_rows, 'tp', 1, 1, tiled=True)  195 us
    all_to_all x2, waiting for transfers between devices, scatter_sum(): received = lax.all_to_all(split_rows, 'tp', 1, 1, tiled=True)  185 us
    all_gather x2, waiting for transfers between devices, device_fn(): full_rows2 = lax.all_gather(normed2, 'tp', axis=1, tiled=True)  92.9 us
    all_gather x2, waiting for transfers between devices, device_fn(): full_rows = lax.all_gather(normed, 'tp', axis=1, tiled=True)  74.9 us
    dot_general x2, matrix products, device_fn(): jnp.einsum('bsf,fd->bsd', hidden, down_weight[layer_idx], preferred_eleme...  51 us
    sub x6, matrix products, doc_causal_attention(): probs_blk = jax.nn.softmax(scores, axis=-1).astype(jnp.bfloat16)  46.2 us
    dot_general x8, matrix products, doc_causal_attention(): jnp.einsum('bhqk,bhke->bqhe', probs_blk, values_in[:, :, :stop_row], pref...  37.3 us
    sub x2, other arithmetic, doc_causal_attention(): probs_blk = jax.nn.softmax(scores, axis=-1).astype(jnp.bfloat16)  32.8 us
  transfers between devices with their start and end apart: 6, of which 6 were waited for; matrix products, arithmetic and copies ran while one was open for 2% of the time, Pallas kernels for 0%

commit v1 on v0

v1 whole, which is shorter than its diff:
```python
import jax
import jax.numpy as jnp
from jax import lax
from jax.experimental import pallas as pl
from jax.experimental.pallas import tpu as pltpu
from jax.sharding import PartitionSpec as P

F32 = jnp.float32
BF16 = jnp.bfloat16
QB = 256
LOG2E = 1.4426950408889634


def layer_norm(residual, gain_vec, shift_vec):
    mean_val = jnp.mean(residual, axis=-1, keepdims=True)
    centered = residual - mean_val
    variance = jnp.mean(centered * centered, axis=-1, keepdims=True)
    return (centered * lax.rsqrt(variance + 1e-5) * gain_vec + shift_vec).astype(BF16)


def attn_kernel(heads, head_dim, qkv_ref, qm_ref, km_ref, out_ref):
    seq = qkv_ref.shape[0]
    width = heads * head_dim
    scale = head_dim ** -0.5 * LOG2E
    row = lax.broadcasted_iota(jnp.int32, (QB, QB), 0)
    col = lax.broadcasted_iota(jnp.int32, (QB, QB), 1)
    diag = jnp.where(col <= row, 0.0, -8e30).astype(F32)
    for i in reversed(range(seq // QB)):
        outs = []
        lo, hi = i * QB, (i + 1) * QB
        for h in range(heads):
            a, b = h * head_dim, (h + 1) * head_dim
            q = jnp.concatenate([qkv_ref[lo:hi, a:b], qm_ref[lo:hi, :]], axis=1)
            k = jnp.concatenate([qkv_ref[0:hi, width + a:width + b], km_ref[0:hi, :]], axis=1)
            s = lax.dot_general(q, k, (((1,), (1,)), ((), ())), preferred_element_type=F32)
            sd = s[:, lo:] + diag
            s = jnp.concatenate([s[:, :lo], sd], axis=1) if i else sd
            m = jnp.max(s, axis=1, keepdims=True)
            e = jnp.exp2((s - m) * scale)
            total = jnp.sum(e, axis=1, keepdims=True)
            p = (e * (1.0 / total)).astype(BF16)
            outs.append(jnp.dot(p, qkv_ref[0:hi, 2 * width + a:2 * width + b], preferred_element_type=F32))
        out_ref[lo:hi, :] = jnp.concatenate(outs, axis=1).astype(BF16)


def attention(qkv, q_mask, k_mask, heads, head_dim):
    seq = qkv.shape[0]

    def body(*refs):
        attn_kernel(heads, head_dim, *refs)

    vm = pl.BlockSpec(memory_space=pltpu.VMEM)
    return pl.pallas_call(
        body,
        out_shape=jax.ShapeDtypeStruct((seq, heads * head_dim), BF16),
        in_specs=[vm] * 3,
        out_specs=vm,
        name="doc_attention",
        cost_estimate=pl.CostEstimate(flops=20_000_000_000, bytes_accessed=5_000_000, transcendentals=0),
        compiler_params=pltpu.CompilerParams(vmem_limit_bytes=48 * 1024 * 1024),
    )(qkv, q_mask, k_mask)


def scatter_sum(partial_rows, groups):
    seq_len, model_dim = partial_rows.shape
    split_rows = partial_rows.reshape(groups, seq_len // groups, model_dim)
    received = lax.all_to_all(split_rows, "tp", 0, 0, tiled=True)
    return jnp.sum(received, axis=0, dtype=F32)


def solution(mesh):
    groups = mesh.shape["tp"]
    row_spec = P("dp", "tp", None)
    vec_spec = P(None, None)
    in_specs = (row_spec, P("dp", "tp"), vec_spec, vec_spec, P(None, None, None, "tp", None), P(None, "tp", None, None), vec_spec, vec_spec, vec_spec, P(None, None, "tp"), P(None, "tp"), P(None, "tp", None), vec_spec)

    def device_fn(tokens, doc_ids, norm1_gain, norm1_shift, qkv_weight, out_weight, out_bias, norm2_gain, norm2_shift, up_weight, up_bias, down_weight, down_bias):
        layers, model_dim, _, heads, head_dim = qkv_weight.shape
        width = heads * head_dim
        rows = tokens.shape[1]
        all_ids = lax.all_gather(doc_ids[0], "tp", axis=0, tiled=True)
        same = all_ids[:, None] == jnp.arange(head_dim, dtype=jnp.int32)[None, :]
        q_mask = jnp.where(same, -8e30, 0.0).astype(BF16)
        k_mask = jnp.where(same, 0.0, 1.0).astype(BF16)
        w_out = lax.all_gather(out_weight.reshape(layers, width, model_dim), "tp", axis=0, tiled=False)
        residual = tokens[0].astype(F32)
        for layer_idx in range(layers):
            normed = layer_norm(residual, norm1_gain[layer_idx], norm1_shift[layer_idx])
            full_rows = lax.all_gather(normed, "tp", axis=0, tiled=True)
            w_qkv = qkv_weight[layer_idx].reshape(model_dim, 3 * width)
            qkv = jnp.dot(full_rows, w_qkv, preferred_element_type=F32).astype(BF16)
            attn_out = attention(qkv, q_mask, k_mask, heads, head_dim)
            mine = lax.all_to_all(attn_out.reshape(groups, rows, width), "tp", 0, 0, tiled=True)
            parts = jnp.einsum("gsk,gkd->gsd", mine, w_out[:, layer_idx], preferred_element_type=F32).astype(BF16)
            residual = residual + (jnp.sum(parts, axis=0, dtype=F32) + out_bias[layer_idx])
            normed2 = layer_norm(residual, norm2_gain[layer_idx], norm2_shift[layer_idx])
            full_rows2 = lax.all_gather(normed2, "tp", axis=0, tiled=True)
            pre_act = jnp.dot(full_rows2, up_weight[layer_idx], preferred_element_type=F32) + up_bias[layer_idx]
            hidden = jax.nn.gelu(pre_act, approximate=True).astype(BF16)
            mlp_part = jnp.dot(hidden, down_weight[layer_idx], preferred_element_type=F32).astype(BF16)
            residual = residual + (scatter_sum(mlp_part, groups) + down_bias[layer_idx])
        return residual.astype(BF16)[None]

    return jax.shard_map(device_fn, mesh=mesh, in_specs=in_specs, out_specs=row_spec, check_vma=False)
```

time: 856 us -> 642 us (0.75)
  matrix products: 176 us -> 83.8 us
  blocking collectives: 207 us -> 129 us
  other arithmetic: 67.5 us -> 22.8 us
  Pallas kernels: 0 us -> 44.6 us
  waiting for transfers between devices: 353 us -> 324 us
    all_to_all x2, blocking collectives: 195 us -> 116 us  [the longest x1 97.8 us: scatter_sum(): received = lax.all_to_all(split_rows, 'tp', 0, 0, tiled=True)]
    all_to_all x2, waiting for transfers between devices: 185 us -> 120 us  [the longest x1 93.6 us: scatter_sum(): received = lax.all_to_all(split_rows, 'tp', 0, 0, tiled=True)]
    sub x6 -> x0, matrix products: 46.2 us -> none  [doc_causal_attention(): probs_blk = jax.nn.softmax(scores, axis=-1).astype(jnp.bfloat16)]
    pallas_call x0 -> x2, Pallas kernels: none -> 44.6 us  [attention(): pl.pallas_call(body, out_shape=jax.ShapeDtypeStruct((seq, heads * head_di...]
    all_gather x4 -> x5, waiting for transfers between devices: 168 us -> 203 us  [the longest x2 94 us: device_fn(): full_rows2 = lax.all_gather(normed2, 'tp', axis=0, tiled=True)]
    sub x2 -> x0, other arithmetic: 32.8 us -> none  [doc_causal_attention(): probs_blk = jax.nn.softmax(scores, axis=-1).astype(jnp.bfloat16)]
    dot_general x14 -> x6, matrix products: 111 us -> 83.8 us  [the longest x2 51 us: device_fn(): jnp.dot(hidden, down_weight[layer_idx], preferred_element_type=F32)]
    unnamed x2 -> x0, matrix products: 18.3 us -> none
  transfers between devices with their start and end apart: 6 -> 7, of which waited for: 6 -> 7; matrix products, arithmetic and copies ran while one was open for 2% -> 3% of each run, Pallas kernels for 0% -> 4%
where the time goes in v1:
time: 642 us; the launch traced here: 638 us
  waiting for transfers between devices  324 us (50%)
  blocking collectives  129 us (20%)
  matrix products  83.8 us (13%)
  Pallas kernels  44.6 us (7%)
  other arithmetic  22.8 us (4%)
  between operations  13.9 us (2%)
  local copies, waits for them, and re-layouts  10.7 us (2%)
  starting transfers between devices  9.19 us (1%)
    all_to_all x1, blocking collectives, scatter_sum(): received = lax.all_to_all(split_rows, 'tp', 0, 0, tiled=True)  97.8 us
    all_gather x2, waiting for transfers between devices, device_fn(): full_rows2 = lax.all_gather(normed2, 'tp', axis=0, tiled=True)  94 us
    all_to_all x1, waiting for transfers between devices, scatter_sum(): received = lax.all_to_all(split_rows, 'tp', 0, 0, tiled=True)  93.6 us
    all_gather x2, waiting for transfers between devices, device_fn(): full_rows = lax.all_gather(normed, 'tp', axis=0, tiled=True)  77.6 us
    dot_general x2, matrix products, device_fn(): jnp.dot(hidden, down_weight[layer_idx], preferred_element_type=F32)  51 us
    pallas_call x2, Pallas kernels, attention(): pl.pallas_call(body, out_shape=jax.ShapeDtypeStruct((seq, heads * head_di...  44.6 us
    all_gather x1, waiting for transfers between devices, device_fn(): lax.all_gather(out_weight.reshape(layers, width, model_dim), 'tp', axis=0...  31.4 us
    all_to_all x1, waiting for transfers between devices, device_fn(): lax.all_to_all(attn_out.reshape(groups, rows, width), 'tp', 0, 0, tiled=T...  26.4 us
  transfers between devices with their start and end apart: 7, of which 7 were waited for; matrix products, arithmetic and copies ran while one was open for 3% of the time, Pallas kernels for 4%

profile of v1, /device:TPU:81, one launch (start us, length us, event | category | flops | bytes accessed | tf_op | source)
XLA Modules:
  0.0 637.6 jit_solution(12059966566106342662)
XLA Ops:
  6.6 0.8 fusion.74
  7.4 0.8 fusion.75
  8.2 1.4 convert_reduce_fusion.4
  9.6 1.6 fusion.50
  11.3 2.7 fusion.53
  14.0 0.1 all-gather.7.cloned.1.call-update
  14.0 0.1 all-gather.9.cloned.1.call-start
  14.1 0.7 all-gather.9.cloned.1.call-update
  14.8 12.3 %all-gather = s32[1,2048]{1,0:T(1,128)S(1)} all-gather(s32[1,256]{1,0:T(1,128)S(1)} %copy-done.13), channel_id=2, replica_groups=mesh['dp'=4,'tp'=8] {'tp'}, dimensions={1}, use_global_device_ids=true | all-gather | bytes 9216 | tf_op jit(solution)/shard_map/all_gather | solution.py:81
  27.1 0.3 select_convert_fusion
  27.5 6.7 %fusion.69 = (bf16[1,2048,3,4,64]{1,4,3,2,0:T(8,128)(2,1)}, bf16[1,2048,3,4,64]{1,4,3,2,0:T(8,128)(2,1)}) fusion(bf16[2,2048,3,4,64]{1,4,3,2,0:T(8,128)(2,1)} %param.17), kind=kLoop, calls=%fused_computation.99 | loop fusion | bytes 12582912 | tf_op jit(solution)/shard_map/slice | solution.py:90
  34.2 31.0 %all-gather.7.cloned.1.call-done = bf16[2048,2048]{1,0:T(8,128)(2,1)} async-done(((bf16[256,2048]{1,0:T(8,128)(2,1)}), bf16[2048,2048]{1,0:T(8,128)(2,1)}) %all-gather.7.cloned.1.call-update) | async-done | bytes 8388624 | tf_op jit(solution)/shard_map/all_gather | solution.py:89
  65.1 10.6 %convolution_convert_fusion.3.refs_0_ = bf16[2048,768]{1,0:T(8,128)(2,1)S(1)} fusion(bf16[2048,2048]{1,0:T(8,128)(2,1)} %all-gather.7.cloned.1.call-done, bf16[2048,768]{0,1:T(8,128)(2,1)} %bitcast.101), kind=kOutput, calls=%fused_computation.49 | convolution fusion | flops 6444023808 | bytes 14680064 | tf_op jit(solution)/shard_map/dot_general | solution.py:91
  75.8 22.8 %doc_attention.2 = bf16[2048,256]{1,0:T(8,128)(2,1)} custom-call(bf16[2048,768]{1,0:T(8,128)(2,1)S(1)} %convolution_convert_fusion.3.refs_0_, bf16[2048,64]{1,0:T(8,128)(2,1)S(1)} %get-tuple-element.26.refs_1_, bf16[2048,64]{1,0:T(8,128)(2,1)S(1)} %get-tuple-element.25.refs_2_), custom_call_target="tpu_custom_call" | custom-call | flops 20000000000 | bytes 5000000 | tf_op jit(solution)/shard_map/doc_attention/pallas_call | solution.py:53
  98.6 3.7 all-to-all-start
  102.5 26.4 %all-to-all-done = bf16[8,256,256]{2,1,0:T(8,128)(2,1)S(1)} async-done(((bf16[8,256,256]{2,1,0:T(8,128)(2,1)}), bf16[8,256,256]{2,1,0:T(8,128)(2,1)S(1)}, u32[]{:S(2)}, u32[]{:S(2)}) %all-to-all-start) | async-done | bytes 1048608 | tf_op jit(solution)/shard_map/all_to_all | solution.py:93
  128.8 31.4 %all-gather.9.cloned.1.call-done = bf16[8,2,256,2048]{3,2,0,1:T(8,128)(2,1)} async-done(((bf16[1,2,256,2048]{3,2,0,1:T(8,128)(2,1)}), bf16[8,2,256,2048]{3,2,0,1:T(8,128)(2,1)}) %all-gather.9.cloned.1.call-update) | async-done | bytes 16777232 | tf_op jit(solution)/shard_map/all_gather | solution.py:85
  160.3 5.9 convert_reduce_fusion.3
  166.2 0.4 fusion.66
  166.6 0.5 multiply_reduce_fusion.2
  167.1 0.4 copy-done.1
  167.5 1.6 add_convert_fusion.2
  169.1 0.1 all-gather.11.cloned.1.call-update
  169.2 47.1 %all-gather.11.cloned.1.call-done = bf16[2048,2048]{1,0:T(8,128)(2,1)} async-done(((bf16[256,2048]{1,0:T(8,128)(2,1)}), bf16[2048,2048]{1,0:T(8,128)(2,1)}) %all-gather.11.cloned.1.call-update) | async-done | bytes 8388624 | tf_op jit(solution)/shard_map/all_gather | solution.py:97
  216.3 25.7 %convolution_convert_fusion.1 = bf16[2048,2048]{1,0:T(8,128)(2,1)} fusion(bf16[2048,2048]{1,0:T(8,128)(2,1)} %all-gather.11.cloned.1.call-done, bf16[2,1024,2048]{2,1,0:T(8,128)(2,1)} %param.24, f32[1024]{0:T(1024)S(1)} %bitcast.123, bf16[2,2048,1024]{2,1,0:T(8,128)(2,1)} %param.22), kind=kOutput, calls=%fused_computation.27 | convolution fusion | flops 17205035008 | bytes 25169920 | tf_op jit(solution)/shard_map/dot_general | solution.py:100
  242.0 5.3 all-to-all-start.1
  247.3 93.6 %all-to-all-done.1 = bf16[8,256,2048]{2,1,0:T(8,128)(2,1)} async-done(((bf16[8,256,2048]{2,1,0:T(8,128)(2,1)}), bf16[8,256,2048]{2,1,0:T(8,128)(2,1)}, u32[]{:S(2)}, u32[]{:S(2)}) %all-to-all-start.1) | async-done | bytes 8388640 | tf_op jit(solution)/shard_map/all_to_all | solution.py:67
  340.9 5.5 convert_reduce_fusion.2
  346.5 0.8 fusion.68
  347.2 0.6 copy-done.6
  347.8 0.4 multiply_reduce_fusion.1
  348.2 1.0 copy-done.4
  349.1 1.4 add_convert_fusion.1
  350.6 0.1 all-gather.15.cloned.1.call-start
  350.7 46.6 %all-gather.13.cloned.1.call-done = bf16[2048,2048]{1,0:T(8,128)(2,1)} async-done(((bf16[256,2048]{1,0:T(8,128)(2,1)}), bf16[2048,2048]{1,0:T(8,128)(2,1)}) %all-gather.13.cloned.1.call-update) | async-done | bytes 8388624 | tf_op jit(solution)/shard_map/all_gather | solution.py:89
  397.3 10.3 %convolution_convert_fusion.2.refs_0_ = bf16[2048,768]{1,0:T(8,128)(2,1)S(1)} fusion(bf16[2048,2048]{1,0:T(8,128)(2,1)} %all-gather.13.cloned.1.call-done, bf16[2048,768]{0,1:T(8,128)(2,1)} %bitcast.100), kind=kOutput, calls=%fused_computation.48 | convolution fusion | flops 6444023808 | bytes 14680064 | tf_op jit(solution)/shard_map/dot_general | solution.py:91
  407.6 21.8 %doc_attention.3 = bf16[2048,256]{1,0:T(8,128)(2,1)S(1)} custom-call(bf16[2048,768]{1,0:T(8,128)(2,1)S(1)} %convolution_convert_fusion.2.refs_0_, bf16[2048,64]{1,0:T(8,128)(2,1)S(1)} %get-tuple-element.26.refs_1_, bf16[2048,64]{1,0:T(8,128)(2,1)S(1)} %get-tuple-element.25.refs_2_), custom_call_target="tpu_custom_call" | custom-call | flops 20000000000 | bytes 5000000 | tf_op jit(solution)/shard_map/doc_attention/pallas_call | solution.py:53
  429.4 18.6 %all_to_all.20 = bf16[8,256,256]{2,1,0:T(8,128)(2,1)S(1)} all-to-all(bf16[8,256,256]{2,1,0:T(8,128)(2,1)S(1)} %bitcast.97), channel_id=1, replica_groups=mesh['dp'=4,'tp'=8] {'tp'}, dimensions={0} | all-to-all | bytes 2097152 | tf_op jit(solution)/shard_map/all_to_all | solution.py:93
  448.0 6.0 convert_reduce_fusion.1
  454.0 0.4 fusion.67
  454.4 0.4 multiply_reduce_fusion
  454.8 1.4 add_convert_fusion
  456.3 46.9 %all-gather.15.cloned.1.call-done = bf16[2048,2048]{1,0:T(8,128)(2,1)} async-done(((bf16[256,2048]{1,0:T(8,128)(2,1)}), bf16[2048,2048]{1,0:T(8,128)(2,1)}) %all-gather.15.cloned.1.call-update) | async-done | bytes 8388624 | tf_op jit(solution)/shard_map/all_gather | solution.py:97
  503.2 25.3 %convolution_convert_fusion = bf16[2048,2048]{1,0:T(8,128)(2,1)} fusion(bf16[2048,2048]{1,0:T(8,128)(2,1)} %all-gather.15.cloned.1.call-done, bf16[2,1024,2048]{2,1,0:T(8,128)(2,1)} %param.24, f32[1024]{0:T(1024)S(1)} %bitcast.122, bf16[2,2048,1024]{2,1,0:T(8,128)(2,1)} %param.22), kind=kOutput, calls=%fused_computation.26 | convolution fusion | flops 17205035008 | bytes 25169920 | tf_op jit(solution)/shard_map/dot_general | solution.py:100
  528.4 97.8 %all_to_all.21 = bf16[8,256,2048]{2,1,0:T(8,128)(2,1)S(1)} all-to-all(bf16[8,256,2048]{2,1,0:T(8,128)(2,1)} %bitcast.99), channel_id=1, replica_groups=mesh['dp'=4,'tp'=8] {'tp'}, dimensions={0} | all-to-all | bytes 16777216 | tf_op jit(solution)/shard_map/all_to_all | solution.py:67
  626.3 1.8 convert_reduce_fusion
  628.1 0.4 copy-done.7
  628.5 2.1 fusion.57
  (42 shorter events, 0.3 us)
Async XLA Ops:
  6.5 58.6 %all-gather.7.cloned.1.call-start = ((), (), s32[]{:S(2)}) async-start(), calls=%async_computation.4 | async-start | bytes 9437184 | tf_op jit(solution)/shard_map/all_gather | solution.py:89
  9.6 5.2 copy-start.13
  14.0 146.2 %all-gather.9.cloned.1.call-start = ((), (), s32[]{:S(2)}) async-start(), calls=%async_computation.5 | async-start | bytes 18874368 | tf_op jit(solution)/shard_map/all_gather | solution.py:85
  75.8 26.6 %copy-start.8 = (f32[2,2048]{1,0:T(2,128)S(1)}, f32[2,2048]{1,0:T(2,128)}, u32[]{:S(2)}) copy-start(f32[2,2048]{1,0:T(2,128)} %param.19) | copy-start | bytes 49156
  75.8 26.6 %copy-start.9 = (f32[2,2048]{1,0:T(2,128)S(1)}, f32[2,2048]{1,0:T(2,128)}, u32[]{:S(2)}) copy-start(f32[2,2048]{1,0:T(2,128)} %param.20) | copy-start | bytes 49156
  75.8 26.6 %copy-start.10 = (f32[2,2048]{1,0:T(2,128)S(1)}, f32[2,2048]{1,0:T(2,128)}, u32[]{:S(2)}) copy-start(f32[2,2048]{1,0:T(2,128)} %param.21) | copy-start | bytes 49156
  98.6 30.2 %all-to-all-start = ((bf16[8,256,256]{2,1,0:T(8,128)(2,1)}), bf16[8,256,256]{2,1,0:T(8,128)(2,1)S(1)}, u32[]{:S(2)}, u32[]{:S(2)}) async-start(bf16[8,256,256]{2,1,0:T(8,128)(2,1)} %bitcast.5), calls=%async_computation | async-start | bytes 2097152 | tf_op jit(solution)/shard_map/all_to_all | solution.py:93
  102.3 113.9 %all-gather.11.cloned.1.call-start = ((), (), s32[]{:S(2)}) async-start(), calls=%async_computation.6 | async-start | bytes 9437184 | tf_op jit(solution)/shard_map/all_gather | solution.py:97
  102.4 63.7 %copy-start = (bf16[1,256,2048]{2,1,0:T(8,128)(2,1)S(1)}, bf16[1,256,2048]{2,1,0:T(8,128)(2,1)}, u32[]{:S(2)}) copy-start(bf16[1,256,2048]{2,1,0:T(8,128)(2,1)} %param.13) | copy-start | bytes 3145732
  166.1 1.4 copy-start.1
  167.1 2.0 copy-start.12
  242.0 5.3 copy-start.11
  242.0 98.9 %all-to-all-start.1 = ((bf16[8,256,2048]{2,1,0:T(8,128)(2,1)}), bf16[8,256,2048]{2,1,0:T(8,128)(2,1)}, u32[]{:S(2)}, u32[]{:S(2)}) async-start(bf16[8,256,2048]{2,1,0:T(8,128)(2,1)} %bitcast.98), calls=%async_computation.1 | async-start | bytes 16777216 | tf_op jit(solution)/shard_map/all_to_all | solution.py:67
  247.3 150.0 %all-gather.13.cloned.1.call-start = ((), (), s32[]{:S(2)}) async-start(), calls=%async_computation.7 | async-start | bytes 9437184 | tf_op jit(solution)/shard_map/all_gather | solution.py:89
  340.9 5.6 copy-start.2
  346.5 1.4 copy-start.6
  347.8 1.3 copy-start.4
  350.6 152.5 %all-gather.15.cloned.1.call-start = ((), (), s32[]{:S(2)}) async-start(), calls=%async_computation.8 | async-start | bytes 9437184 | tf_op jit(solution)/shard_map/all_gather | solution.py:97
  448.0 6.0 copy-start.5
  626.3 1.8 copy-start.3
  626.3 2.2 copy-start.7
Sparse Core Ops, SparseCore 0:
  14.1 50.9 all-gather.6
  66.7 93.4 all-gather.8
  169.3 46.9 all-gather.10
  350.8 46.5 all-gather.12
  456.4 46.6 all-gather.14

commit v2 on v1

--- a/solution.py
+++ b/solution.py
@@ -61,11 +61,247 @@
     )(qkv, q_mask, k_mask)
 
 
-def scatter_sum(partial_rows, groups):
-    seq_len, model_dim = partial_rows.shape
-    split_rows = partial_rows.reshape(groups, seq_len // groups, model_dim)
-    received = lax.all_to_all(split_rows, "tp", 0, 0, tiled=True)
-    return jnp.sum(received, axis=0, dtype=F32)
+HALF = 128
+CH = 64
+OWN, LEFT, RIGHT, OPP = 0, 1, 2, 3
+MESH_ID = pl.DeviceIdType.MESH
+
+
+class Peers:
+    def __init__(self, n):
+        me = lax.axis_index("tp")
+        chips = n // 2
+        self.k = lax.rem(me, 2)
+        chip = me // 2
+        self.right = lax.rem(chip + 1, chips)
+        self.left = lax.rem(chip + chips - 1, chips)
+        self.chip = chip
+        self.chips = chips
+        self.opp = lax.rem(chip + 2, chips)
+
+    def dev(self, chip, core):
+        return {"tp": 2 * chip + core}
+
+    @property
+    def sib(self):
+        return {"tp": 2 * self.chip + 1 - self.k}
+
+    def greet(self):
+        barrier = pltpu.get_barrier_semaphore()
+        for d in (self.sib, self.dev(self.left, 0), self.dev(self.left, 1), self.dev(self.right, 0), self.dev(self.right, 1)):
+            pl.semaphore_signal(barrier, inc=1, device_id=d, device_id_type=MESH_ID)
+
+    def met(self):
+        pl.semaphore_wait(pltpu.get_barrier_semaphore(), 5)
+
+
+class Copies:
+    def __init__(self):
+        self.sent = []
+
+    def send(self, src, dst, ss, rs, device):
+        c = pltpu.make_async_remote_copy(src_ref=src, dst_ref=dst, send_sem=ss, recv_sem=rs, device_id=device, device_id_type=MESH_ID)
+        c.start()
+        self.sent.append(c)
+
+    def recv(self, dst, ss, rs, device):
+        pltpu.make_async_remote_copy(src_ref=dst, dst_ref=dst, send_sem=ss, recv_sem=rs, device_id=device, device_id_type=MESH_ID).wait_recv()
+
+    def drain(self):
+        for c in self.sent:
+            c.wait_send()
+
+
+class Gather:
+    def __init__(self, peers, copies, buf, ss, rs):
+        self.p, self.c, self.buf, self.ss, self.rs = peers, copies, buf, ss, rs
+
+    def at(self, place, c, core):
+        return self.buf.at[2 * place + c // 2, core, pl.ds((c % 2) * CH, CH), :]
+
+    def start(self, c):
+        p, k = self.p, self.p.k
+        src = self.at(OWN, c, k)
+        self.c.send(src, self.at(LEFT, c, k), self.ss.at[0, c], self.rs.at[0, c], p.dev(p.right, k))
+        self.c.send(src, self.at(RIGHT, c, k), self.ss.at[1, c], self.rs.at[1, c], p.dev(p.left, k))
+        self.c.send(src, src, self.ss.at[2, c], self.rs.at[2, c], p.sib)
+
+    def wait(self, kind, place, c, core):
+        self.c.recv(self.at(place, c, core), self.ss.at[kind, c], self.rs.at[kind, c], self.p.sib)
+
+    def wait_sibling(self, c):
+        self.wait(2, OWN, c, 1 - self.p.k)
+
+    def near(self, c):
+        p, k = self.p, self.p.k
+        self.wait(0, LEFT, c, k)
+        self.wait(1, RIGHT, c, k)
+        self.c.send(self.at(1 + k, c, k), self.at(OPP, c, k), self.ss.at[5, c], self.rs.at[5, c], p.dev(lax.rem(p.chip + p.chips + 1 - 2 * k, p.chips), k))
+        self.c.send(self.at(LEFT, c, k), self.at(LEFT, c, k), self.ss.at[3, c], self.rs.at[3, c], p.sib)
+        self.c.send(self.at(RIGHT, c, k), self.at(RIGHT, c, k), self.ss.at[4, c], self.rs.at[4, c], p.sib)
+
+    def near_sibling(self, c):
+        self.wait(3, LEFT, c, 1 - self.p.k)
+        self.wait(4, RIGHT, c, 1 - self.p.k)
+
+    def far(self, c):
+        k = self.p.k
+        self.wait(5, OPP, c, k)
+        self.c.send(self.at(OPP, c, k), self.at(OPP, c, k), self.ss.at[6, c], self.rs.at[6, c], self.p.sib)
+
+    def far_sibling(self, c):
+        self.wait(6, OPP, c, 1 - self.p.k)
+
+
+def norm_rows(res_ref, gain, shift, buf, k):
+    for c in range(4):
+        x = res_ref[c * CH:(c + 1) * CH, :]
+        mean = jnp.mean(x, axis=1, keepdims=True)
+        cen = x - mean
+        var = jnp.mean(cen * cen, axis=1, keepdims=True)
+        h = (cen * lax.rsqrt(var + 1e-5) * gain + shift).astype(BF16)
+        buf[c // 2, k, pl.ds((c % 2) * CH, CH), :] = h
+
+
+def mlp_kernel(n, layer, res_ref, gain_ref, shift_ref, up_hbm, ub_ref, down_hbm, db_ref, out_ref,
+               buf, part, hid, w_up, w_down, sibp, direct, midr, omid, msum, fin,
+               w_sem, ag_ss, ag_rs, d_ss, d_rs, s_ss, s_rs, m_ss, m_rs, o_ss, o_rs, f_ss, f_rs):
+    p = Peers(n)
+    k = p.k
+    p.greet()
+    load_up = pltpu.make_async_copy(up_hbm.at[layer], w_up, w_sem.at[0])
+    load_down = pltpu.make_async_copy(down_hbm.at[layer], w_down, w_sem.at[1])
+    load_up.start()
+    load_down.start()
+    norm_rows(res_ref, gain_ref[layer:layer + 1, :], shift_ref[layer:layer + 1, :], buf, k)
+    copies = Copies()
+    g = Gather(p, copies, buf, ag_ss, ag_rs)
+    p.met()
+    for c in range(4):
+        g.start(c)
+    load_up.wait()
+    load_down.wait()
+    ff = w_up.shape[1]
+    dm = w_down.shape[1]
+    UN, DN = 512, 512
+    rows = 2 * HALF
+
+    def unit(u):
+        def up(j, _):
+            cols = pl.ds(pl.multiple_of(j * UN, UN), UN)
+            x = buf[u].reshape(rows, dm)
+            a = jnp.dot(x, w_up[:, cols], preferred_element_type=F32) + ub_ref[layer:layer + 1, cols]
+            cdf = 0.5 * (1.0 + jnp.tanh(0.7978845608028654 * (a + 0.044715 * (a * a * a))))
+            hid[:, cols] = (a * cdf).astype(BF16)
+            return 0
+
+        def down(j, _):
+            cols = pl.ds(pl.multiple_of(j * DN, DN), DN)
+            y = jnp.dot(hid[...], w_down[:, cols], preferred_element_type=F32).astype(BF16)
+            part[u, :, :, cols] = y.reshape(2, HALF, DN)
+            return 0
+
+        lax.fori_loop(0, ff // UN, up, 0)
+        lax.fori_loop(0, dm // DN, down, 0)
+
+    def pair(s):
+        def one(i, _):
+            unit(2 + s + 2 * i)
+            return 0
+        lax.fori_loop(0, 2, one, 0)
+
+    def send_direct(s):
+        copies.send(part.at[2 * RIGHT + s, 1], direct.at[k, s], d_ss.at[0, s], d_rs.at[k, s], p.dev(p.right, 1))
+        copies.send(part.at[2 * LEFT + s, 0], direct.at[k, s], d_ss.at[1, s], d_rs.at[k, s], p.dev(p.left, 0))
+
+    for c in range(4):
+        g.wait_sibling(c)
+    unit(0)
+    g.near(0)
+    unit(1)
+    g.near(1)
+    for s in range(2):
+        copies.send(part.at[s, 1 - k], sibp.at[s], s_ss.at[s], s_rs.at[s], p.sib)
+    g.near_sibling(0)
+    g.near_sibling(1)
+    pair(0)
+    g.near(2)
+    g.near(3)
+    send_direct(0)
+    g.near_sibling(2)
+    g.near_sibling(3)
+    pair(1)
+    send_direct(1)
+    copies.send(part.at[2 * RIGHT + 1 - k, 0], midr.at[0], m_ss.at[0], m_rs.at[0], p.sib)
+    copies.send(part.at[2 * LEFT + 1 - k, 1], midr.at[1], m_ss.at[1], m_rs.at[1], p.sib)
+    for s in range(2):
+        g.far(2 * s)
+        g.far(2 * s + 1)
+        g.far_sibling(2 * s)
+        g.far_sibling(2 * s + 1)
+        unit(2 * OPP + s)
+        for j in range(2):
+            r = pl.ds(j * CH, CH)
+            copies.send(part.at[2 * OPP + s, 0, r, :], omid.at[0, k, r, :], o_ss.at[0, s, j], o_rs.at[0, k, j], p.dev(p.right, s))
+            copies.send(part.at[2 * OPP + s, 1, r, :], omid.at[1, k, r, :], o_ss.at[1, s, j], o_rs.at[1, k, j], p.dev(p.left, s))
+    for e in range(2):
+        copies.recv(midr.at[e], m_ss.at[e], m_rs.at[e], p.sib)
+    for j in range(2):
+        r = pl.ds(j * CH, CH)
+        for e in range(2):
+            for q in range(2):
+                copies.recv(omid.at[e, q, r, :], o_ss.at[e, q, j], o_rs.at[e, q, j], p.sib)
+            own = part[2 * (RIGHT if e == 0 else LEFT) + k, e, r, :].astype(F32)
+            msum[e, r, :] = (own + midr[e, r, :].astype(F32)) + (omid[e, 0, r, :].astype(F32) + omid[e, 1, r, :].astype(F32))
+            copies.send(msum.at[e, r, :], fin.at[k, r, :], f_ss.at[e, j], f_rs.at[k, j], p.dev(p.right, 0) if e == 0 else p.dev(p.left, 1))
+    for s in range(2):
+        copies.recv(sibp.at[s], s_ss.at[s], s_rs.at[s], p.sib)
+        for q in range(2):
+            copies.recv(direct.at[q, s], d_ss.at[q, s], d_rs.at[q, s], p.sib)
+    for j in range(2):
+        r = pl.ds(j * CH, CH)
+        for s in range(2):
+            copies.recv(fin.at[s, r, :], f_ss.at[s, j], f_rs.at[s, j], p.sib)
+            total = (part[s, k, r, :].astype(F32) + sibp[s, r, :].astype(F32)) + (direct[0, s, r, :].astype(F32) + direct[1, s, r, :].astype(F32)) + fin[s, r, :]
+            o = pl.ds(s * HALF + j * CH, CH)
+            out_ref[o, :] = res_ref[o, :] + (total + db_ref[layer:layer + 1, :])
+    copies.drain()
+
+
+def mlp(n, layer, residual, gain, shift, up_w, up_b, down_w, down_b):
+    rows, dm = residual.shape
+    ff = up_w.shape[2]
+
+    def body(*refs):
+        mlp_kernel(n, layer, *refs)
+
+    vm = pl.BlockSpec(memory_space=pltpu.VMEM)
+    hb = pl.BlockSpec(memory_space=pl.ANY)
+    dma = pltpu.SemaphoreType.DMA
+    return pl.pallas_call(
+        body,
+        out_shape=jax.ShapeDtypeStruct((rows, dm), F32),
+        in_specs=[vm, vm, vm, hb, vm, hb, vm],
+        out_specs=vm,
+        scratch_shapes=[
+            pltpu.VMEM((8, 2, HALF, dm), BF16),
+            pltpu.VMEM((8, 2, HALF, dm), BF16),
+            pltpu.VMEM((2 * HALF, ff), BF16),
+            pltpu.VMEM((dm, ff), BF16),
+            pltpu.VMEM((ff, dm), BF16),
+            pltpu.VMEM((2, HALF, dm), BF16),
+            pltpu.VMEM((2, 2, HALF, dm), BF16),
+            pltpu.VMEM((2, HALF, dm), BF16),
+            pltpu.VMEM((2, 2, HALF, dm), BF16),
+            pltpu.VMEM((2, HALF, dm), F32),
+            pltpu.VMEM((2, HALF, dm), F32),
+            dma((2,)), dma((7, 4)), dma((7, 4)), dma((2, 2)), dma((2, 2)), dma((2,)), dma((2,)), dma((2,)), dma((2,)),
+            dma((2, 2, 2)), dma((2, 2, 2)), dma((2, 2)), dma((2, 2)),
+        ],
+        name=f"mlp_{layer}",
+        cost_estimate=pl.CostEstimate(flops=80_000_000_000, bytes_accessed=20_000_000, transcendentals=0),
+        compiler_params=pltpu.CompilerParams(collective_id=10 + layer, has_side_effects=True, vmem_limit_bytes=60 * 1024 * 1024),
+    )(residual, gain, shift, up_w, up_b, down_w, down_b)
 
 
 def solution(mesh):
@@ -93,12 +329,7 @@
             mine = lax.all_to_all(attn_out.reshape(groups, rows, width), "tp", 0, 0, tiled=True)
             parts = jnp.einsum("gsk,gkd->gsd", mine, w_out[:, layer_idx], preferred_element_type=F32).astype(BF16)
             residual = residual + (jnp.sum(parts, axis=0, dtype=F32) + out_bias[layer_idx])
-            normed2 = layer_norm(residual, norm2_gain[layer_idx], norm2_shift[layer_idx])
-            full_rows2 = lax.all_gather(normed2, "tp", axis=0, tiled=True)
-            pre_act = jnp.dot(full_rows2, up_weight[layer_idx], preferred_element_type=F32) + up_bias[layer_idx]
-            hidden = jax.nn.gelu(pre_act, approximate=True).astype(BF16)
-            mlp_part = jnp.dot(hidden, down_weight[layer_idx], preferred_element_type=F32).astype(BF16)
-            residual = residual + (scatter_sum(mlp_part, groups) + down_bias[layer_idx])
+            residual = mlp(groups, layer_idx, residual, norm2_gain, norm2_shift, up_weight, up_bias, down_weight, down_bias)
         return residual.astype(BF16)[None]
 
     return jax.shard_map(device_fn, mesh=mesh, in_specs=in_specs, out_specs=row_spec, check_vma=False)

time: 642 us -> 508 us (0.79)
  Pallas kernels: 44.6 us -> 262 us
  waiting for transfers between devices: 324 us -> 137 us
  blocking collectives: 129 us -> 30.9 us
  matrix products: 83.8 us -> 32.3 us
  other arithmetic: 22.8 us -> 14.7 us
    pallas_call x0 -> x2, Pallas kernels: none -> 217 us  [mlp(): pl.pallas_call(body, out_shape=jax.ShapeDtypeStruct((rows, dm), F32), in_...]
    all_to_all x1 -> x0, blocking collectives: 97.8 us -> none  [scatter_sum(): received = lax.all_to_all(split_rows, 'tp', 0, 0, tiled=True)]
    all_gather x2 -> x0, waiting for transfers between devices: 94 us -> none  [device_fn(): full_rows2 = lax.all_gather(normed2, 'tp', axis=0, tiled=True)]
    all_to_all x1 -> x0, waiting for transfers between devices: 93.6 us -> none  [scatter_sum(): received = lax.all_to_all(split_rows, 'tp', 0, 0, tiled=True)]
    dot_general x2 -> x0, matrix products: 51 us -> none  [device_fn(): jnp.dot(hidden, down_weight[layer_idx], preferred_element_type=F32)]
    reduce_sum x2 -> x0, other arithmetic: 7.35 us -> none  [scatter_sum(): return jnp.sum(received, axis=0, dtype=F32)]
  transfers between devices with their start and end apart: 7 -> 4, of which waited for: 7 -> 4; matrix products, arithmetic and copies ran while one was open for 3% -> 3% of each run, Pallas kernels for 4% -> 5%
where the time goes in v2:
time: 508 us; the launch traced here: 503 us
  Pallas kernels  262 us (52%)
  waiting for transfers between devices  137 us (27%)
  matrix products  32.3 us (6%)
  blocking collectives  30.9 us (6%)
  other arithmetic  14.7 us (3%)
  between operations  13.7 us (3%)
  local copies, waits for them, and re-layouts  8.63 us (2%)
    pallas_call x2, Pallas kernels, mlp(): pl.pallas_call(body, out_shape=jax.ShapeDtypeStruct((rows, dm), F32), in_...  217 us
    all_gather x2, waiting for transfers between devices, device_fn(): full_rows = lax.all_gather(normed, 'tp', axis=0, tiled=True)  78.1 us
    pallas_call x2, Pallas kernels, attention(): pl.pallas_call(body, out_shape=jax.ShapeDtypeStruct((seq, heads * head_di...  44.6 us
    all_gather x1, waiting for transfers between devices, device_fn(): lax.all_gather(out_weight.reshape(layers, width, model_dim), 'tp', axis=0...  31.7 us
    all_to_all x1, waiting for transfers between devices, device_fn(): lax.all_to_all(attn_out.reshape(groups, rows, width), 'tp', 0, 0, tiled=T...  26.4 us
    dot_general x2, matrix products, device_fn(): qkv = jnp.dot(full_rows, w_qkv, preferred_element_type=F32).astype(BF16)  20.5 us
    all_to_all x1, blocking collectives, device_fn(): lax.all_to_all(attn_out.reshape(groups, rows, width), 'tp', 0, 0, tiled=T...  18.6 us
    all_gather x1, blocking collectives, device_fn(): all_ids = lax.all_gather(doc_ids[0], 'tp', axis=0, tiled=True)  12.3 us
  transfers between devices with their start and end apart: 4, of which 4 were waited for; matrix products, arithmetic and copies ran while one was open for 3% of the time, Pallas kernels for 5%

profile of v2, /device:TPU:81, one launch (start us, length us, event | category | flops | bytes accessed | tf_op | source)
XLA Modules:
  0.0 503.0 jit_solution(13507682607289071682)
XLA Ops:
  6.5 0.0 copy-start.1
  6.5 0.0 all-gather.5.cloned.1.call-start
  6.6 0.8 fusion.12
  7.4 0.8 fusion.13
  8.2 1.4 convert_reduce_fusion.2
  9.7 1.6 fusion.6
  11.3 0.0 copy-done.1
  11.3 1.4 fusion.9
  12.8 0.0 copy-start.3
  12.8 0.1 all-gather.5.cloned.1.call-update
  12.8 0.1 all-gather.7.cloned.1.call-start
  12.9 0.7 all-gather.7.cloned.1.call-update
  13.6 0.0 copy-done.3
  13.6 12.3 %all-gather = s32[1,2048]{1,0:T(1,128)S(1)} all-gather(s32[1,256]{1,0:T(1,128)S(1)} %copy-done.3), channel_id=2, replica_groups=mesh['dp'=4,'tp'=8] {'tp'}, dimensions={1}, use_global_device_ids=true | all-gather | bytes 9216 | tf_op jit(solution)/shard_map/all_gather | solution.py:317
  25.9 0.3 select_convert_fusion
  26.3 6.7 %fusion.10 = (bf16[1,2048,3,4,64]{1,4,3,2,0:T(8,128)(2,1)}, bf16[1,2048,3,4,64]{1,4,3,2,0:T(8,128)(2,1)}) fusion(bf16[2,2048,3,4,64]{1,4,3,2,0:T(8,128)(2,1)} %param.17), kind=kLoop, calls=%fused_computation.29 | loop fusion | bytes 12582912 | tf_op jit(solution)/shard_map/slice | solution.py:326
  33.0 31.0 %all-gather.5.cloned.1.call-done = bf16[2048,2048]{1,0:T(8,128)(2,1)} async-done(((bf16[256,2048]{1,0:T(8,128)(2,1)}), bf16[2048,2048]{1,0:T(8,128)(2,1)}) %all-gather.5.cloned.1.call-update) | async-done | bytes 8388624 | tf_op jit(solution)/shard_map/all_gather | solution.py:325
  63.9 10.3 %convolution_convert_fusion.1.refs_0_ = bf16[2048,768]{1,0:T(8,128)(2,1)S(1)} fusion(bf16[2048,2048]{1,0:T(8,128)(2,1)} %all-gather.5.cloned.1.call-done, bf16[2048,768]{0,1:T(8,128)(2,1)} %bitcast.50), kind=kOutput, calls=%fused_computation.7 | convolution fusion | flops 6444023808 | bytes 14680064 | tf_op jit(solution)/shard_map/dot_general | solution.py:327
  74.2 22.8 %doc_attention.2 = bf16[2048,256]{1,0:T(8,128)(2,1)} custom-call(bf16[2048,768]{1,0:T(8,128)(2,1)S(1)} %convolution_convert_fusion.1.refs_0_, bf16[2048,64]{1,0:T(8,128)(2,1)S(1)} %get-tuple-element.14.refs_1_, bf16[2048,64]{1,0:T(8,128)(2,1)S(1)} %get-tuple-element.13.refs_2_), custom_call_target="tpu_custom_call" | custom-call | flops 20000000000 | bytes 5000000 | tf_op jit(solution)/shard_map/doc_attention/pallas_call | solution.py:53
  97.0 0.0 copy-start.2
  97.0 3.9 all-to-all-start
  100.9 0.0 all-gather.9.cloned.1.call-start
  100.9 0.0 copy-done.2
  100.9 26.4 %all-to-all-done = bf16[8,256,256]{2,1,0:T(8,128)(2,1)S(1)} async-done(((bf16[8,256,256]{2,1,0:T(8,128)(2,1)}), bf16[8,256,256]{2,1,0:T(8,128)(2,1)S(1)}, u32[]{:S(2)}, u32[]{:S(2)}) %all-to-all-start) | async-done | bytes 1048608 | tf_op jit(solution)/shard_map/all_to_all | solution.py:329
  127.3 31.7 %all-gather.7.cloned.1.call-done = bf16[8,2,256,2048]{3,2,0,1:T(8,128)(2,1)} async-done(((bf16[1,2,256,2048]{3,2,0,1:T(8,128)(2,1)}), bf16[8,2,256,2048]{3,2,0,1:T(8,128)(2,1)}) %all-gather.7.cloned.1.call-update) | async-done | bytes 16777232 | tf_op jit(solution)/shard_map/all_gather | solution.py:321
  159.1 5.9 %convert_reduce_fusion.1 = f32[256,2048]{1,0:T(8,128)S(1)} fusion(bf16[8,256,256]{2,1,0:T(8,128)(2,1)S(1)} %all-to-all-done, bf16[8,2,256,2048]{3,2,0,1:T(8,128)(2,1)} %all-gather.7.cloned.1.call-done), kind=kOutput, calls=%fused_computation.1 | convolution fusion | flops 2159542272 | bytes 11534336 | tf_op jit(solution)/shard_map/gsk,gkd->gsd/dot_general | solution.py:330
  164.9 1.7 fusion.2.refs_0_
  166.6 108.3 %mlp_0.1 = f32[256,2048]{1,0:T(8,128)} custom-call(f32[256,2048]{1,0:T(8,128)} %fusion.2.refs_0_, f32[2,2048]{1,0:T(2,128)} %refs_1_.3, f32[2,2048]{1,0:T(2,128)} %refs_2_.3, bf16[2,2048,1024]{2,1,0:T(8,128)(2,1)} %refs_3_.3, f32[2,1024]{1,0:T(2,128)} %refs_4_.3, bf16[2,1024,2048]{2,1,0:T(8,128)(2,1)} %refs_5_.3, f32[2,2048]{1,0:T(2,128)} %refs_6_.3), custom_call_target="tpu_custom_call" | custom-call | flops 80000000000 | bytes 20000000 | tf_op jit(solution)/shard_map/mlp_0/pallas_call | solution.py:281
  274.9 0.0 copy-start
  274.9 1.9 reduce_sum.57
  276.9 0.3 copy-done
  277.1 0.3 multiply_reduce_fusion
  277.5 1.4 add_convert_fusion
  278.9 0.1 all-gather.9.cloned.1.call-update
  279.0 47.2 %all-gather.9.cloned.1.call-done = bf16[2048,2048]{1,0:T(8,128)(2,1)} async-done(((bf16[256,2048]{1,0:T(8,128)(2,1)}), bf16[2048,2048]{1,0:T(8,128)(2,1)}) %all-gather.9.cloned.1.call-update) | async-done | bytes 8388624 | tf_op jit(solution)/shard_map/all_gather | solution.py:325
  326.1 10.3 %convolution_convert_fusion.refs_0_ = bf16[2048,768]{1,0:T(8,128)(2,1)S(1)} fusion(bf16[2048,2048]{1,0:T(8,128)(2,1)} %all-gather.9.cloned.1.call-done, bf16[2048,768]{0,1:T(8,128)(2,1)} %bitcast.49), kind=kOutput, calls=%fused_computation.6 | convolution fusion | flops 6444023808 | bytes 14680064 | tf_op jit(solution)/shard_map/dot_general | solution.py:327
  336.4 21.8 %doc_attention.3 = bf16[2048,256]{1,0:T(8,128)(2,1)S(1)} custom-call(bf16[2048,768]{1,0:T(8,128)(2,1)S(1)} %convolution_convert_fusion.refs_0_, bf16[2048,64]{1,0:T(8,128)(2,1)S(1)} %get-tuple-element.14.refs_1_, bf16[2048,64]{1,0:T(8,128)(2,1)S(1)} %get-tuple-element.13.refs_2_), custom_call_target="tpu_custom_call" | custom-call | flops 20000000000 | bytes 5000000 | tf_op jit(solution)/shard_map/doc_attention/pallas_call | solution.py:53
  358.2 18.6 %all_to_all.10 = bf16[8,256,256]{2,1,0:T(8,128)(2,1)S(1)} all-to-all(bf16[8,256,256]{2,1,0:T(8,128)(2,1)S(1)} %bitcast.48), channel_id=1, replica_groups=mesh['dp'=4,'tp'=8] {'tp'}, dimensions={0} | all-to-all | bytes 2097152 | tf_op jit(solution)/shard_map/all_to_all | solution.py:329
  376.8 5.9 %convert_reduce_fusion = f32[256,2048]{1,0:T(8,128)S(1)} fusion(bf16[8,256,256]{2,1,0:T(8,128)(2,1)S(1)} %all_to_all.10, bf16[8,2,256,2048]{3,2,0,1:T(8,128)(2,1)} %all-gather.7.cloned.1.call-done), kind=kOutput, calls=%fused_computation | convolution fusion | flops 2159542272 | bytes 11534336 | tf_op jit(solution)/shard_map/gsk,gkd->gsd/dot_general | solution.py:330
  382.7 1.7 add_add_fusion.refs_0_
  384.4 108.9 %mlp_1.1 = f32[256,2048]{1,0:T(8,128)} custom-call(f32[256,2048]{1,0:T(8,128)} %add_add_fusion.refs_0_, f32[2,2048]{1,0:T(2,128)} %refs_1_.3, f32[2,2048]{1,0:T(2,128)} %refs_2_.3, bf16[2,2048,1024]{2,1,0:T(8,128)(2,1)} %refs_3_.3, f32[2,1024]{1,0:T(2,128)} %refs_4_.3, bf16[2,1024,2048]{2,1,0:T(8,128)(2,1)} %refs_5_.3, f32[2,2048]{1,0:T(2,128)} %refs_6_.3), custom_call_target="tpu_custom_call" | custom-call | flops 80000000000 | bytes 20000000 | tf_op jit(solution)/shard_map/mlp_1/pallas_call | solution.py:281
  493.3 2.7 convert_bitcast_fusion.1
  (5 shorter events, 0.0 us)
Async XLA Ops:
  6.5 4.8 copy-start.1
  6.5 57.4 %all-gather.5.cloned.1.call-start = ((), (), s32[]{:S(2)}) async-start(), calls=%async_computation.2 | async-start | bytes 9437184 | tf_op jit(solution)/shard_map/all_gather | solution.py:325
  12.8 0.9 copy-start.3
  12.8 146.2 %all-gather.7.cloned.1.call-start = ((), (), s32[]{:S(2)}) async-start(), calls=%async_computation.3 | async-start | bytes 18874368 | tf_op jit(solution)/shard_map/all_gather | solution.py:321
  97.0 3.9 copy-start.2
  97.0 30.3 %all-to-all-start = ((bf16[8,256,256]{2,1,0:T(8,128)(2,1)}), bf16[8,256,256]{2,1,0:T(8,128)(2,1)S(1)}, u32[]{:S(2)}, u32[]{:S(2)}) async-start(bf16[8,256,256]{2,1,0:T(8,128)(2,1)} %bitcast.5), calls=%async_computation | async-start | bytes 2097152 | tf_op jit(solution)/shard_map/all_to_all | solution.py:329
  100.9 225.3 %all-gather.9.cloned.1.call-start = ((), (), s32[]{:S(2)}) async-start(), calls=%async_computation.4 | async-start | bytes 9437184 | tf_op jit(solution)/shard_map/all_gather | solution.py:325
  274.9 2.2 copy-start
Sparse Core Ops, SparseCore 0:
  12.9 50.9 all-gather.4
  65.5 93.4 all-gather.6
  279.1 46.9 all-gather.8

commit v3 on v2

--- a/solution.py
+++ b/solution.py
@@ -7,60 +7,6 @@
 
 F32 = jnp.float32
 BF16 = jnp.bfloat16
-QB = 256
-LOG2E = 1.4426950408889634
-
-
-def layer_norm(residual, gain_vec, shift_vec):
-    mean_val = jnp.mean(residual, axis=-1, keepdims=True)
-    centered = residual - mean_val
-    variance = jnp.mean(centered * centered, axis=-1, keepdims=True)
-    return (centered * lax.rsqrt(variance + 1e-5) * gain_vec + shift_vec).astype(BF16)
-
-
-def attn_kernel(heads, head_dim, qkv_ref, qm_ref, km_ref, out_ref):
-    seq = qkv_ref.shape[0]
-    width = heads * head_dim
-    scale = head_dim ** -0.5 * LOG2E
-    row = lax.broadcasted_iota(jnp.int32, (QB, QB), 0)
-    col = lax.broadcasted_iota(jnp.int32, (QB, QB), 1)
-    diag = jnp.where(col <= row, 0.0, -8e30).astype(F32)
-    for i in reversed(range(seq // QB)):
-        outs = []
-        lo, hi = i * QB, (i + 1) * QB
-        for h in range(heads):
-            a, b = h * head_dim, (h + 1) * head_dim
-            q = jnp.concatenate([qkv_ref[lo:hi, a:b], qm_ref[lo:hi, :]], axis=1)
-            k = jnp.concatenate([qkv_ref[0:hi, width + a:width + b], km_ref[0:hi, :]], axis=1)
-            s = lax.dot_general(q, k, (((1,), (1,)), ((), ())), preferred_element_type=F32)
-            sd = s[:, lo:] + diag
-            s = jnp.concatenate([s[:, :lo], sd], axis=1) if i else sd
-            m = jnp.max(s, axis=1, keepdims=True)
-            e = jnp.exp2((s - m) * scale)
-            total = jnp.sum(e, axis=1, keepdims=True)
-            p = (e * (1.0 / total)).astype(BF16)
-            outs.append(jnp.dot(p, qkv_ref[0:hi, 2 * width + a:2 * width + b], preferred_element_type=F32))
-        out_ref[lo:hi, :] = jnp.concatenate(outs, axis=1).astype(BF16)
-
-
-def attention(qkv, q_mask, k_mask, heads, head_dim):
-    seq = qkv.shape[0]
-
-    def body(*refs):
-        attn_kernel(heads, head_dim, *refs)
-
-    vm = pl.BlockSpec(memory_space=pltpu.VMEM)
-    return pl.pallas_call(
-        body,
-        out_shape=jax.ShapeDtypeStruct((seq, heads * head_dim), BF16),
-        in_specs=[vm] * 3,
-        out_specs=vm,
-        name="doc_attention",
-        cost_estimate=pl.CostEstimate(flops=20_000_000_000, bytes_accessed=5_000_000, transcendentals=0),
-        compiler_params=pltpu.CompilerParams(vmem_limit_bytes=48 * 1024 * 1024),
-    )(qkv, q_mask, k_mask)
-
-
 HALF = 128
 CH = 64
 OWN, LEFT, RIGHT, OPP = 0, 1, 2, 3
@@ -91,6 +37,15 @@
         for d in (self.sib, self.dev(self.left, 0), self.dev(self.left, 1), self.dev(self.right, 0), self.dev(self.right, 1)):
             pl.semaphore_signal(barrier, inc=1, device_id=d, device_id_type=MESH_ID)
 
+    def greet_all(self, n):
+        barrier = pltpu.get_barrier_semaphore()
+        for d in range(1, n):
+            other = lax.rem(2 * self.chip + self.k + d, n)
+            pl.semaphore_signal(barrier, inc=1, device_id={"tp": other}, device_id_type=MESH_ID)
+
+    def met_all(self, n):
+        pl.semaphore_wait(pltpu.get_barrier_semaphore(), n - 1)
+
     def met(self):
         pl.semaphore_wait(pltpu.get_barrier_semaphore(), 5)
 
@@ -155,7 +110,7 @@
 
 def norm_rows(res_ref, gain, shift, buf, k):
     for c in range(4):
-        x = res_ref[c * CH:(c + 1) * CH, :]
+        x = res_ref[c * CH:(c + 1) * CH, :].astype(F32)
         mean = jnp.mean(x, axis=1, keepdims=True)
         cen = x - mean
         var = jnp.mean(cen * cen, axis=1, keepdims=True)
@@ -304,6 +259,230 @@
     )(residual, gain, shift, up_w, up_b, down_w, down_b)
 
 
+QB = 256
+LOG2E = 1.4426950408889634
+PAD = 128
+
+
+def attn_kernel(n, layer, res_ref, gain_ref, shift_ref, hot_ref, qkv_hbm, wo_hbm, ob_ref, out_ref,
+                buf, wbuf, w_qk, w_v, qk_s, v_s, qm_s, km_s, hots, heads_s, got,
+                w_sem, h_ss, h_rs, ag_ss, ag_rs, wg_ss, wg_rs, a_ss, a_rs):
+    p = Peers(n)
+    k = p.k
+    me = 2 * p.chip + k
+    heads, dim = qkv_hbm.shape[2], qkv_hbm.shape[3]
+    dm = res_ref.shape[1]
+    width = heads * dim
+    rows = 2 * HALF
+    scale = dim ** -0.5 * LOG2E
+    p.greet_all(n)
+    loads = []
+    for t in range(2):
+        for h in range(heads):
+            loads.append(pltpu.make_async_copy(qkv_hbm.at[layer, t, h], w_qk.at[t * heads + h, 0:dim, :], w_sem.at[t * heads + h]))
+    for h in range(heads):
+        loads.append(pltpu.make_async_copy(qkv_hbm.at[layer, 2, h], w_v.at[pl.ds(h * dim, dim), :], w_sem.at[2 * heads + h]))
+    wloads = [pltpu.make_async_copy(wo_hbm.at[layer, pl.ds(s * HALF, HALF), :], wbuf.at[s, k], w_sem.at[3 * heads + s]) for s in range(2)]
+    for c in loads + wloads:
+        c.start()
+    norm_rows(res_ref, gain_ref[layer:layer + 1, :], shift_ref[layer:layer + 1, :], buf, k)
+    for t in range(2 * heads):
+        w_qk[t, dim:PAD, :] = jnp.zeros((PAD - dim, dm), BF16)
+    hots[me] = hot_ref[...]
+    copies = Copies()
+    g = Gather(p, copies, buf, ag_ss, ag_rs)
+    gw = Gather(p, copies, wbuf, wg_ss, wg_rs)
+    p.met_all(n)
+    for d in range(1, n):
+        copies.send(hot_ref, hots.at[me], h_ss.at[d - 1], h_rs.at[d - 1], {"tp": lax.rem(me + d, n)})
+    for c in range(4):
+        g.start(c)
+    for c in loads + wloads:
+        c.wait()
+    for d in range(1, n):
+        src = lax.rem(me + n - d, n)
+        copies.recv(hots.at[src], h_ss.at[d - 1], h_rs.at[d - 1], p.sib)
+    docs = hot_ref.shape[0]
+    lane = lax.broadcasted_iota(jnp.int32, (docs, PAD), 1)
+    place = lax.broadcasted_iota(jnp.int32, (docs, PAD), 0)
+    pick = jnp.where(lane == place + dim, 1.0, 0.0).astype(BF16)
+    lanes = lax.broadcasted_iota(jnp.int32, (QB, PAD), 1)
+    used = jnp.where((lanes >= dim) & (lanes < dim + docs), 1.0, 0.0).astype(F32)
+    for i in range(n):
+        one = lax.dot_general(hots[i], pick, (((0,), (0,)), ((), ())), preferred_element_type=F32)
+        qm_s[i * QB:(i + 1) * QB, :] = (one * -8e30).astype(BF16)
+        km_s[i * QB:(i + 1) * QB, :] = (used - one).astype(BF16)
+
+    def unit(u, chip):
+        x = buf[u].reshape(rows, dm)
+        half = u % 2 if isinstance(u, int) else lax.rem(u, 2)
+        for t in range(2):
+            w = w_qk[t * heads:(t + 1) * heads].reshape(heads * PAD, dm)
+            y = lax.dot_general(x, w, (((1,), (1,)), ((), ())), preferred_element_type=F32)
+            for kk in range(2):
+                at = pl.ds(pl.multiple_of((2 * chip + kk) * rows + half * HALF, HALF), HALF)
+                mask = (qm_s if t == 0 else km_s)[at, :].astype(F32)
+                for h in range(heads):
+                    part = y[kk * HALF:(kk + 1) * HALF, h * PAD:(h + 1) * PAD] + mask
+                    qk_s[at, (t * heads + h) * PAD:(t * heads + h + 1) * PAD] = part.astype(BF16)
+        y = lax.dot_general(x, w_v[...], (((1,), (1,)), ((), ())), preferred_element_type=F32).astype(BF16)
+        for kk in range(2):
+            at = pl.ds(pl.multiple_of((2 * chip + kk) * rows + half * HALF, HALF), HALF)
+            v_s[at, :] = y[kk * HALF:(kk + 1) * HALF, :]
+
+    def pair(s):
+        def one(i, _):
+            unit(2 + s + 2 * i, p.left + i * (p.right - p.left))
+            return 0
+        lax.fori_loop(0, 2, one, 0)
+
+    for c in range(4):
+        g.wait_sibling(c)
+    unit(0, p.chip)
+    g.near(0)
+    unit(1, p.chip)
+    g.near(1)
+    g.near_sibling(0)
+    g.near_sibling(1)
+    pair(0)
+    g.near(2)
+    g.near(3)
+    for c in range(4):
+        gw.start(c)
+    g.near_sibling(2)
+    g.near_sibling(3)
+    pair(1)
+    for s in range(2):
+        g.far(2 * s)
+        g.far(2 * s + 1)
+        g.far_sibling(2 * s)
+        g.far_sibling(2 * s + 1)
+        unit(2 * OPP + s, p.opp)
+
+    row = lax.broadcasted_iota(jnp.int32, (QB, QB), 0)
+    col = lax.broadcasted_iota(jnp.int32, (QB, QB), 1)
+    diag = jnp.where(col <= row, 0.0, -8e30).astype(F32)
+    low = lax.broadcasted_iota(jnp.int32, (1, PAD), 1) < dim
+
+    def block(i):
+        lo, hi = i * QB, (i + 1) * QB
+        for gr in range(heads // 2):
+            pair_v = v_s[0:hi, gr * PAD:(gr + 1) * PAD]
+            zero = jnp.zeros_like(pair_v)
+            out = None
+            for b in range(2):
+                h = 2 * gr + b
+                q = qk_s[lo:hi, h * PAD:(h + 1) * PAD]
+                kk = qk_s[0:hi, (heads + h) * PAD:(heads + h + 1) * PAD]
+                s = lax.dot_general(q, kk, (((1,), (1,)), ((), ())), preferred_element_type=F32)
+                sd = s[:, lo:] + diag
+                s = jnp.concatenate([s[:, :lo], sd], axis=1) if i else sd
+                m = jnp.max(s, axis=1, keepdims=True)
+                e = jnp.exp2((s - m) * scale)
+                total = jnp.sum(e, axis=1, keepdims=True)
+                pr = (e * (1.0 / total)).astype(BF16)
+                v = jnp.where(low, pair_v, zero) if b == 0 else jnp.where(low, zero, pair_v)
+                o = jnp.dot(pr, v, preferred_element_type=F32)
+                out = o if out is None else out + o
+            heads_s[i, :, gr * PAD:(gr + 1) * PAD] = out.astype(BF16)
+
+    def to_owner(i):
+        return pltpu.make_async_remote_copy(src_ref=heads_s.at[i], dst_ref=got.at[me], send_sem=a_ss.at[i], recv_sem=a_rs.at[me], device_id={"tp": i}, device_id_type=MESH_ID)
+
+    for i in range(n):
+        block(i)
+
+        @pl.when(me != i)
+        def _():
+            to_owner(i).start()
+
+        if i == n // 2 - 1:
+            gw.near(0)
+        elif i == n - 3:
+            gw.near(1)
+        elif i == n - 2:
+            gw.near(2)
+    for c in range(4):
+        gw.wait_sibling(c)
+    gw.near(3)
+    got[me] = heads_s[me]
+    out_ref[...] = jnp.zeros_like(out_ref)
+    DN = 512
+
+    def project(o, chip, core):
+        a = got[2 * chip + core]
+
+        def tile(j, _):
+            cols = pl.ds(pl.multiple_of(j * DN, DN), DN)
+            w = wbuf[2 * o:2 * o + 2, core, :, cols].reshape(rows, DN)
+            out_ref[:, cols] += jnp.dot(a, w, preferred_element_type=F32).astype(BF16).astype(F32)
+            return 0
+
+        lax.fori_loop(0, dm // DN, tile, 0)
+
+    def arrive(src):
+        pltpu.make_async_remote_copy(src_ref=got.at[src], dst_ref=got.at[src], send_sem=a_ss.at[src], recv_sem=a_rs.at[src], device_id=p.sib, device_id_type=MESH_ID).wait_recv()
+
+    arrive(2 * p.chip + 1 - k)
+    for kk in range(2):
+        project(OWN, p.chip, kk)
+    for c in range(4):
+        gw.near_sibling(c)
+    for o, chip in ((LEFT, p.left), (RIGHT, p.right)):
+        for kk in range(2):
+            arrive(2 * chip + kk)
+            project(o, chip, kk)
+    for c in range(4):
+        gw.far(c)
+    for c in range(4):
+        gw.far_sibling(c)
+    for kk in range(2):
+        arrive(2 * p.opp + kk)
+        project(OPP, p.opp, kk)
+    out_ref[...] = res_ref[...].astype(F32) + (out_ref[...] + ob_ref[layer:layer + 1, :])
+    copies.drain()
+    for i in range(n):
+        @pl.when(me != i)
+        def _():
+            to_owner(i).wait_send()
+
+
+def attn_block(n, layer, residual, gain, shift, hot, qkv_w, out_w, out_b):
+    rows, dm = residual.shape
+    heads, dim = qkv_w.shape[2], qkv_w.shape[3]
+    seq = n * rows
+
+    def body(*refs):
+        attn_kernel(n, layer, *refs)
+
+    vm = pl.BlockSpec(memory_space=pltpu.VMEM)
+    hb = pl.BlockSpec(memory_space=pl.ANY)
+    dma = pltpu.SemaphoreType.DMA
+    return pl.pallas_call(
+        body,
+        out_shape=jax.ShapeDtypeStruct((rows, dm), F32),
+        in_specs=[vm, vm, vm, vm, hb, hb, vm],
+        out_specs=vm,
+        scratch_shapes=[
+            pltpu.VMEM((8, 2, HALF, dm), BF16),
+            pltpu.VMEM((8, 2, HALF, dm), BF16),
+            pltpu.VMEM((2 * heads, PAD, dm), BF16),
+            pltpu.VMEM((heads * dim, dm), BF16),
+            pltpu.VMEM((seq, 2 * heads * PAD), BF16),
+            pltpu.VMEM((seq, heads * dim), BF16),
+            pltpu.VMEM((seq, PAD), BF16),
+            pltpu.VMEM((seq, PAD), BF16),
+            pltpu.VMEM((n,) + hot.shape, BF16),
+            pltpu.VMEM((n, rows, heads * dim), BF16),
+            pltpu.VMEM((n, rows, heads * dim), BF16),
+            dma((3 * heads + 2,)), dma((n - 1,)), dma((n - 1,)), dma((7, 4)), dma((7, 4)), dma((7, 4)), dma((7, 4)), dma((n,)), dma((n,)),
+        ],
+        name=f"attn_{layer}",
+        cost_estimate=pl.CostEstimate(flops=60_000_000_000, bytes_accessed=20_000_000, transcendentals=0),
+        compiler_params=pltpu.CompilerParams(collective_id=20 + layer, has_side_effects=True, vmem_limit_bytes=62 * 1024 * 1024),
+    )(residual, gain, shift, hot, qkv_w, out_w, out_b)
+
+
 def solution(mesh):
     groups = mesh.shape["tp"]
     row_spec = P("dp", "tp", None)
@@ -312,24 +491,13 @@
 
     def device_fn(tokens, doc_ids, norm1_gain, norm1_shift, qkv_weight, out_weight, out_bias, norm2_gain, norm2_shift, up_weight, up_bias, down_weight, down_bias):
         layers, model_dim, _, heads, head_dim = qkv_weight.shape
-        width = heads * head_dim
-        rows = tokens.shape[1]
-        all_ids = lax.all_gather(doc_ids[0], "tp", axis=0, tiled=True)
-        same = all_ids[:, None] == jnp.arange(head_dim, dtype=jnp.int32)[None, :]
-        q_mask = jnp.where(same, -8e30, 0.0).astype(BF16)
-        k_mask = jnp.where(same, 0.0, 1.0).astype(BF16)
-        w_out = lax.all_gather(out_weight.reshape(layers, width, model_dim), "tp", axis=0, tiled=False)
-        residual = tokens[0].astype(F32)
-        for layer_idx in range(layers):
-            normed = layer_norm(residual, norm1_gain[layer_idx], norm1_shift[layer_idx])
-            full_rows = lax.all_gather(normed, "tp", axis=0, tiled=True)
-            w_qkv = qkv_weight[layer_idx].reshape(model_dim, 3 * width)
-            qkv = jnp.dot(full_rows, w_qkv, preferred_element_type=F32).astype(BF16)
-            attn_out = attention(qkv, q_mask, k_mask, heads, head_dim)
-            mine = lax.all_to_all(attn_out.reshape(groups, rows, width), "tp", 0, 0, tiled=True)
-            parts = jnp.einsum("gsk,gkd->gsd", mine, w_out[:, layer_idx], preferred_element_type=F32).astype(BF16)
-            residual = residual + (jnp.sum(parts, axis=0, dtype=F32) + out_bias[layer_idx])
-            residual = mlp(groups, layer_idx, residual, norm2_gain, norm2_shift, up_weight, up_bias, down_weight, down_bias)
+        hot = (jnp.arange(16, dtype=jnp.int32)[:, None] == doc_ids).astype(BF16)
+        qkv_t = jnp.transpose(qkv_weight, (0, 2, 3, 4, 1))
+        out_w = out_weight.reshape(layers, heads * head_dim, model_dim)
+        residual = tokens[0]
+        for layer in range(layers):
+            residual = attn_block(groups, layer, residual, norm1_gain, norm1_shift, hot, qkv_t, out_w, out_bias)
+            residual = mlp(groups, layer, residual, norm2_gain, norm2_shift, up_weight, up_bias, down_weight, down_bias)
         return residual.astype(BF16)[None]
 
     return jax.shard_map(device_fn, mesh=mesh, in_specs=in_specs, out_specs=row_spec, check_vma=False)

time: 508 us -> 418 us (0.82)
  Pallas kernels: 262 us -> 405 us
  waiting for transfers between devices: 137 us -> 0 us
  matrix products: 32.3 us -> 0 us
  blocking collectives: 30.9 us -> 0 us
  between operations: 13.7 us -> 0.47 us
  other arithmetic: 14.7 us -> 4 us
  local copies, waits for them, and re-layouts: 8.63 us -> 0 us
    pallas_call x2, Pallas kernels: 44.6 us -> 187 us  [attn_block(): pl.pallas_call(body, out_shape=jax.ShapeDtypeStruct((rows, dm), F32), in_...]
    all_gather x3 -> x0, waiting for transfers between devices: 110 us -> none  [the longest x2 78.1 us: device_fn(): full_rows = lax.all_gather(normed, 'tp', axis=0, tiled=True)]
    dot_general x4 -> x0, matrix products: 32.3 us -> none  [the longest x2 20.5 us: device_fn(): qkv = jnp.dot(full_rows, w_qkv, preferred_element_type=F32).astype(BF16)]
    all_to_all x1 -> x0, waiting for transfers between devices: 26.4 us -> none  [device_fn(): lax.all_to_all(attn_out.reshape(groups, rows, width), 'tp', 0, 0, tiled=T...]
    all_to_all x1 -> x0, blocking collectives: 18.6 us -> none  [device_fn(): lax.all_to_all(attn_out.reshape(groups, rows, width), 'tp', 0, 0, tiled=T...]
    all_gather x1 -> x0, blocking collectives: 12.3 us -> none  [device_fn(): all_ids = lax.all_gather(doc_ids[0], 'tp', axis=0, tiled=True)]
    slice x4 -> x0, local copies, waits for them, and re-layouts: 8.34 us -> none  [the longest x1 6.67 us: device_fn(): w_qkv = qkv_weight[layer_idx].reshape(model_dim, 3 * width)]
    reduce_sum x4 -> x0, other arithmetic: 5.35 us -> none  [the longest x2 3.36 us: layer_norm(): mean_val = jnp.mean(residual, axis=-1, keepdims=True)]
  transfers between devices with their start and end apart: 4 -> 0, of which waited for: 4 -> 0; matrix products, arithmetic and copies ran while one was open for 3% -> 0% of each run, Pallas kernels for 5% -> 0%
where the time goes in v3:
time: 418 us; the launch traced here: 409 us
  Pallas kernels  405 us (97%)
    pallas_call x2, Pallas kernels, mlp(): pl.pallas_call(body, out_shape=jax.ShapeDtypeStruct((rows, dm), F32), in_...  218 us
    pallas_call x2, Pallas kernels, attn_block(): pl.pallas_call(body, out_shape=jax.ShapeDtypeStruct((rows, dm), F32), in_...  187 us

profile of v3, /device:TPU:81, one launch (start us, length us, event | category | flops | bytes accessed | tf_op | source)
XLA Modules:
  0.0 409.4 jit_solution(3532132707456288147)
XLA Ops:
  0.0 1.3 fusion.refs_3_
  1.3 93.2 %attn_0.1.refs_0_ = f32[256,2048]{1,0:T(8,128)} custom-call(bf16[256,2048]{1,0:T(8,128)(2,1)} %bitcast.11, f32[2,2048]{1,0:T(2,128)} %refs_1_.6, f32[2,2048]{1,0:T(2,128)} %refs_2_.6, bf16[16,256]{1,0:T(8,128)(2,1)} %fusion.refs_3_, bf16[2,3,4,64,2048]{4,3,2,1,0:T(8,128)(2,1)} %bitcast.7, bf16[2,256,2048]{2,1,0:T(8,128)(2,1)} %bitcast.9, f32[2,2048]{1,0:T(2,128)} %refs_6_.6), custom_call_target="tpu_custom_call" | custom-call | flops 60000002048 | bytes 20000000 | tf_op jit(solution)/shard_map/attn_0/pallas_call | solution.py:461
  94.5 108.9 %mlp_0.1.refs_0_ = f32[256,2048]{1,0:T(8,128)} custom-call(f32[256,2048]{1,0:T(8,128)} %attn_0.1.refs_0_, f32[2,2048]{1,0:T(2,128)} %refs_1_.7, f32[2,2048]{1,0:T(2,128)} %refs_2_.7, bf16[2,2048,1024]{2,1,0:T(8,128)(2,1)} %refs_3_.3, f32[2,1024]{1,0:T(2,128)} %refs_4_.3, bf16[2,1024,2048]{2,1,0:T(8,128)(2,1)} %refs_5_.3, f32[2,2048]{1,0:T(2,128)} %refs_6_.7), custom_call_target="tpu_custom_call" | custom-call | flops 80000000000 | bytes 20000000 | tf_op jit(solution)/shard_map/mlp_0/pallas_call | solution.py:236
  203.4 93.7 %attn_1.1.refs_0_ = f32[256,2048]{1,0:T(8,128)} custom-call(f32[256,2048]{1,0:T(8,128)} %mlp_0.1.refs_0_, f32[2,2048]{1,0:T(2,128)} %refs_1_.6, f32[2,2048]{1,0:T(2,128)} %refs_2_.6, bf16[16,256]{1,0:T(8,128)(2,1)} %fusion.refs_3_, bf16[2,3,4,64,2048]{4,3,2,1,0:T(8,128)(2,1)} %bitcast.8, bf16[2,256,2048]{2,1,0:T(8,128)(2,1)} %bitcast.10, f32[2,2048]{1,0:T(2,128)} %refs_6_.6), custom_call_target="tpu_custom_call" | custom-call | flops 60000002048 | bytes 20000000 | tf_op jit(solution)/shard_map/attn_1/pallas_call | solution.py:461
  297.1 109.1 %mlp_1.1 = f32[256,2048]{1,0:T(8,128)} custom-call(f32[256,2048]{1,0:T(8,128)} %attn_1.1.refs_0_, f32[2,2048]{1,0:T(2,128)} %refs_1_.7, f32[2,2048]{1,0:T(2,128)} %refs_2_.7, bf16[2,2048,1024]{2,1,0:T(8,128)(2,1)} %refs_3_.3, f32[2,1024]{1,0:T(2,128)} %refs_4_.3, bf16[2,1024,2048]{2,1,0:T(8,128)(2,1)} %refs_5_.3, f32[2,2048]{1,0:T(2,128)} %refs_6_.7), custom_call_target="tpu_custom_call" | custom-call | flops 80000000000 | bytes 20000000 | tf_op jit(solution)/shard_map/mlp_1/pallas_call | solution.py:236
  406.3 2.7 convert_bitcast_fusion

commit v4 on v0

v4 whole, which is shorter than its diff:
```python
import jax
import jax.numpy as jnp
from jax import lax
from jax.experimental import pallas as pl
from jax.experimental.pallas import tpu as pltpu
from jax.sharding import PartitionSpec as P

F32 = jnp.float32
BF16 = jnp.bfloat16
HALF = 128
CH = 64
WCH = 32
QB = 256
PAD = 128
LOG2E = 1.4426950408889634
OWN, LEFT, RIGHT, OPP = 0, 1, 2, 3
MESH_ID = pl.DeviceIdType.MESH


def slot(place, s):
    return {OWN: s, LEFT: 2 + 2 * s, RIGHT: 3 + 2 * s, OPP: 6 + s}[place]


class Peers:
    def __init__(self, n):
        self.n = n
        self.me = lax.axis_index("tp")
        chips = n // 2
        self.k = lax.rem(self.me, 2)
        self.chip = self.me // 2
        self.right = lax.rem(self.chip + 1, chips)
        self.left = lax.rem(self.chip + chips - 1, chips)
        self.opp = lax.rem(self.chip + 2, chips)
        self.onward = lax.rem(self.chip + chips + 1 - 2 * self.k, chips)
        dp = lax.axis_index("dp")
        self.side = lax.rem(dp, 2)
        self.twin = {"dp": dp + 1 - 2 * self.side, "tp": self.me}
        self.sib = {"tp": 2 * self.chip + 1 - self.k}
        self.to_right = [{"tp": 2 * self.right + c} for c in (0, 1)]
        self.to_left = [{"tp": 2 * self.left + c} for c in (0, 1)]
        self.same_right = {"tp": 2 * self.right + self.k}
        self.same_left = {"tp": 2 * self.left + self.k}
        self.same_onward = {"tp": 2 * self.onward + self.k}


    def greet(self, sem):
        for d in range(1, self.n):
            pl.semaphore_signal(sem, inc=1, device_id={"tp": lax.rem(self.me + d, self.n)}, device_id_type=MESH_ID)
        pl.semaphore_signal(sem, inc=1, device_id=self.twin, device_id_type=MESH_ID)

    def met(self, sem):
        pl.semaphore_wait(sem, self.n)


def copy(src, dst, ss, rs, device):
    return pltpu.make_async_remote_copy(src_ref=src, dst_ref=dst, send_sem=ss, recv_sem=rs, device_id=device, device_id_type=MESH_ID)


class Copies:
    def __init__(self, p):
        self.p = p
        self.sent = []

    def send(self, make):
        make().start()
        self.sent.append(make)

    def recv(self, dst, ss, rs):
        copy(dst, dst, ss, rs, self.p.sib).wait_recv()

    def drain(self):
        for make in self.sent:
            make().wait_send()
        self.sent = []


class Gather(Copies):
    def __init__(self, p, buf, ss, rs):
        super().__init__(p)
        self.buf, self.ss, self.rs = buf, ss, rs

    def at(self, place, c, core):
        return self.buf.at[slot(place, c // 2), core, pl.ds((c % 2) * CH, CH), :]

    def put(self, kind, c, src, dst, device):
        self.send(lambda: copy(src(), dst(), self.ss.at[kind, c], self.rs.at[kind, c], device))

    def take(self, kind, place, c, core):
        self.recv(self.at(place, c, core), self.ss.at[kind, c], self.rs.at[kind, c])

    def start(self, c):
        p, k = self.p, self.p.k
        own = lambda: self.at(OWN, c, k)
        self.put(0, c, own, lambda: self.at(LEFT, c, k), p.same_right)
        self.put(1, c, own, lambda: self.at(RIGHT, c, k), p.same_left)
        self.put(2, c, own, own, p.sib)

    def sibling(self, c):
        self.take(2, OWN, c, 1 - self.p.k)

    def near(self, c):
        p, k = self.p, self.p.k
        self.take(0, LEFT, c, k)
        self.take(1, RIGHT, c, k)
        ring = lambda: self.buf.at[2 + 2 * (c // 2) + k, k, pl.ds((c % 2) * CH, CH), :]
        self.put(5, c, ring, lambda: self.at(OPP, c, k), p.same_onward)
        self.put(3, c, lambda: self.at(LEFT, c, k), lambda: self.at(LEFT, c, k), p.sib)
        self.put(4, c, lambda: self.at(RIGHT, c, k), lambda: self.at(RIGHT, c, k), p.sib)

    def near_sibling(self, c):
        self.take(3, LEFT, c, 1 - self.p.k)
        self.take(4, RIGHT, c, 1 - self.p.k)

    def far(self, c):
        k = self.p.k
        self.take(5, OPP, c, k)
        self.put(6, c, lambda: self.at(OPP, c, k), lambda: self.at(OPP, c, k), self.p.sib)

    def far_sibling(self, c):
        self.take(6, OPP, c, 1 - self.p.k)


class WeightGather(Copies):
    def __init__(self, p, buf, ss, rs):
        super().__init__(p)
        self.buf, self.ss, self.rs = buf, ss, rs

    def mine(self, i):
        return i + 5 * self.p.side if i < 3 else i

    def theirs(self, i):
        return i + 5 * (1 - self.p.side)

    def at_slot(self, spot, c, core):
        start = (c % (HALF // WCH)) * WCH
        if not isinstance(start, int):
            start = pl.multiple_of(start, WCH)
        return self.buf.at[spot, core, pl.ds(start, WCH), :]

    def at(self, place, c, core):
        return self.at_slot(slot(place, c // (HALF // WCH)), c, core)

    def put(self, kind, c, src, dst, device):
        self.send(lambda: copy(src(c()), dst(c()), self.ss.at[kind, c()], self.rs.at[kind, c()], device))

    def take(self, kind, place, c, core):
        self.recv(self.at(place, c, core), self.ss.at[kind, c], self.rs.at[kind, c])

    def start(self):
        p, k = self.p, self.p.k
        for i in range(5):
            c = lambda i=i: self.mine(i)
            self.put(0, c, lambda c: self.at(OWN, c, k), lambda c: self.at(LEFT, c, k), p.same_right)
            self.put(1, c, lambda c: self.at(OWN, c, k), lambda c: self.at(RIGHT, c, k), p.same_left)
        for s in range(2):
            self.send(lambda s=s: copy(self.buf.at[s, k], self.buf.at[s, k], self.ss.at[2, s], self.rs.at[2, s], p.sib))

    def sibling(self):
        for s in range(2):
            self.recv(self.buf.at[s, 1 - self.p.k], self.ss.at[2, s], self.rs.at[2, s])

    def near(self, i):
        p, k = self.p, self.p.k
        c = lambda: self.mine(i)
        left = lambda c: self.at(LEFT, c, k)
        right = lambda c: self.at(RIGHT, c, k)
        self.take(0, LEFT, c(), k)
        self.take(1, RIGHT, c(), k)
        ring = lambda c: self.at_slot(2 + 2 * (c // (HALF // WCH)) + k, c, k)
        self.put(5, c, ring, lambda c: self.at(OPP, c, k), p.same_onward)
        if i < 3:
            self.put(7, c, left, left, p.twin)
            self.put(8, c, right, right, p.twin)
        self.put(3, c, left, left, p.sib)
        self.put(4, c, right, right, p.sib)

    def far(self, i):
        p, k = self.p, self.p.k
        c = lambda: self.mine(i)
        opp = lambda c: self.at(OPP, c, k)
        self.take(5, OPP, c(), k)
        if i < 3:
            self.put(9, c, opp, opp, p.twin)
        self.put(6, c, opp, opp, p.sib)

    def twin_near(self, i):
        p, k = self.p, self.p.k
        c = lambda: self.theirs(i)
        left = lambda c: self.at(LEFT, c, k)
        right = lambda c: self.at(RIGHT, c, k)
        self.take(7, LEFT, c(), k)
        self.take(8, RIGHT, c(), k)
        self.put(3, c, left, left, p.sib)
        self.put(4, c, right, right, p.sib)

    def twin_far(self, i):
        p, k = self.p, self.p.k
        c = lambda: self.theirs(i)
        opp = lambda c: self.at(OPP, c, k)
        self.take(9, OPP, c(), k)
        self.put(6, c, opp, opp, p.sib)

    def near_sibling(self):
        for c in range(8):
            self.take(3, LEFT, c, 1 - self.p.k)
            self.take(4, RIGHT, c, 1 - self.p.k)

    def far_sibling(self):
        for c in range(8):
            self.take(6, OPP, c, 1 - self.p.k)


def run_steps(unit, before, after):
    def step(i, _):
        for j, f in before.items():
            pl.when(i == j)(f)
        unit(i)
        for j, f in after.items():
            pl.when(i == j)(f)
        return 0

    lax.fori_loop(0, 8, step, 0)


def kernel(n, tok_ref, hot_ref, n1g, n1s, qkv_hbm, wo_hbm, ob_ref, n2g, n2s, up_hbm, ub_ref, down_hbm, db_ref, out_ref,
           res, buf, big, w_qk, w_v, w_up, w_down, qk_s, v_s, qm_s, km_s, hots, heads_s, got,
           hid, sibp, direct, midr, omid, msum, fin,
           w_sem, turn, h_ss, h_rs, ag_ss, ag_rs, wg_ss, wg_rs, mg_ss, mg_rs, a_ss, a_rs,
           d_ss, d_rs, s_ss, s_rs, m_ss, m_rs, o_ss, o_rs, f_ss, f_rs):
    p = Peers(n)
    k, me = p.k, p.me
    layers, _, heads, dim, dm = qkv_hbm.shape
    ff = w_up.shape[1]
    rows = 2 * HALF
    scale = dim ** -0.5 * LOG2E
    entry = pltpu.get_barrier_semaphore()
    p.greet(entry)

    def qkv_loads(l):
        out = []
        for t in range(2):
            for h in range(heads):
                out.append(pltpu.make_async_copy(qkv_hbm.at[l, t, h], w_qk.at[t * heads + h, 0:dim, :], w_sem.at[t * heads + h]))
        for h in range(heads):
            out.append(pltpu.make_async_copy(qkv_hbm.at[l, 2, h], w_v.at[pl.ds(h * dim, dim), :], w_sem.at[2 * heads + h]))
        return out

    def out_loads(l):
        return [pltpu.make_async_copy(wo_hbm.at[l, pl.ds(s * HALF, HALF), :], big.at[s, k], w_sem.at[3 * heads + s]) for s in range(2)]

    def mlp_loads(l):
        up = pltpu.make_async_copy(up_hbm.at[l], w_up, w_sem.at[3 * heads + 2])
        return [up, pltpu.make_async_copy(down_hbm.at[l], w_down, w_sem.at[3 * heads + 3])]

    for c in qkv_loads(0):
        c.start()
    for t in range(2 * heads):
        w_qk[t, dim:PAD, :] = jnp.zeros((PAD - dim, dm), BF16)
    hots[me] = hot_ref[...]

    def widen(c, _):
        r = pl.ds(pl.multiple_of(c * CH, CH), CH)
        res[r, :] = tok_ref[r, :].astype(F32)
        return 0

    lax.fori_loop(0, 4, widen, 0)

    def norm_rows(gain, shift):
        def part(c, _):
            x = res[pl.ds(pl.multiple_of(c * CH, CH), CH), :]
            cen = x - jnp.mean(x, axis=1, keepdims=True)
            var = jnp.mean(cen * cen, axis=1, keepdims=True)
            h = (cen * lax.rsqrt(var + 1e-5) * gain + shift).astype(BF16)
            buf[c // 2, k, pl.ds(pl.multiple_of((c % 2) * CH, CH), CH), :] = h
            return 0

        lax.fori_loop(0, 4, part, 0)

    docs = hot_ref.shape[0]
    lanes = lax.broadcasted_iota(jnp.int32, (QB, PAD), 1)
    row = lax.broadcasted_iota(jnp.int32, (QB, QB), 0)
    col = lax.broadcasted_iota(jnp.int32, (QB, QB), 1)
    low = lax.broadcasted_iota(jnp.int32, (1, PAD), 1) < dim

    def masks():
        for d in range(1, n):
            src = lax.rem(me + n - d, n)
            copy(hots.at[src], hots.at[src], h_ss.at[d - 1], h_rs.at[d - 1], p.sib).wait_recv()
        lane = lax.broadcasted_iota(jnp.int32, (docs, PAD), 1)
        place = lax.broadcasted_iota(jnp.int32, (docs, PAD), 0)
        pick = jnp.where(lane == place + dim, 1.0, 0.0).astype(BF16)
        used = jnp.where((lanes >= dim) & (lanes < dim + docs), 1.0, 0.0).astype(F32)

        def one(i, _):
            x = lax.dot_general(hots[i], pick, (((0,), (0,)), ((), ())), preferred_element_type=F32)
            r = pl.ds(pl.multiple_of(i * QB, QB), QB)
            qm_s[r, :] = (x * -8e30).astype(BF16)
            km_s[r, :] = (used - x).astype(BF16)
            return 0

        lax.fori_loop(0, n, one, 0)

    def layer(l, _):
        at_l = pl.ds(l, 1)
        for c in out_loads(l) + mlp_loads(l):
            c.start()
        norm_rows(n1g[at_l, :], n1s[at_l, :])

        @pl.when(l == 0)
        def _():
            p.met(entry)
            for d in range(1, n):
                copy(hot_ref, hots.at[me], h_ss.at[d - 1], h_rs.at[d - 1], {"tp": lax.rem(me + d, n)}).start()

        @pl.when(l > 0)
        def _():
            p.met(turn)

        g = Gather(p, buf, ag_ss, ag_rs)
        gw = WeightGather(p, big, wg_ss, wg_rs)
        for c in range(4):
            g.start(c)
        for c in qkv_loads(l):
            c.wait()
        pl.when(l == 0)(masks)

        def project_in(i):
            x = buf[i].reshape(rows, dm)
            middle = (i >= 2) & (i < 6)
            half = jnp.where(middle, i // 2 - 1, lax.rem(i, 2))
            chip = jnp.where(i < 2, p.chip, jnp.where(middle, jnp.where(lax.rem(i, 2) == 0, p.left, p.right), p.opp))
            spots = [pl.ds(pl.multiple_of((2 * chip + kk) * rows + half * HALF, HALF), HALF) for kk in range(2)]
            for t in range(2):
                w = w_qk[t * heads:(t + 1) * heads].reshape(heads * PAD, dm)
                y = lax.dot_general(x, w, (((1,), (1,)), ((), ())), preferred_element_type=F32)
                for kk in range(2):
                    mask = (qm_s if t == 0 else km_s)[spots[kk], :].astype(F32)
                    for h in range(heads):
                        part = y[kk * HALF:(kk + 1) * HALF, h * PAD:(h + 1) * PAD] + mask
                        qk_s[spots[kk], (t * heads + h) * PAD:(t * heads + h + 1) * PAD] = part.astype(BF16)
            y = lax.dot_general(x, w_v[...], (((1,), (1,)), ((), ())), preferred_element_type=F32).astype(BF16)
            for kk in range(2):
                v_s[spots[kk], :] = y[kk * HALF:(kk + 1) * HALF, :]

        def arrivals(gg):
            def four():
                gg.near_sibling(2)
                gg.near_sibling(3)

            def six():
                for c in (0, 1):
                    gg.far(c)
                for c in (0, 1):
                    gg.far_sibling(c)

            def seven():
                for c in (2, 3):
                    gg.far(c)
                for c in (2, 3):
                    gg.far_sibling(c)

            def zero():
                gg.sibling(0)
                gg.sibling(1)

            def one():
                gg.sibling(2)
                gg.sibling(3)

            def two():
                gg.near_sibling(0)
                gg.near_sibling(1)

            return {0: zero, 1: one, 2: two, 4: four, 6: six, 7: seven}

        def after_three():
            g.near(2)
            g.near(3)
            for c in out_loads(l):
                c.wait()
            gw.start()

        run_steps(project_in, arrivals(g), {0: lambda: g.near(0), 1: lambda: g.near(1), 3: after_three})
        g.drain()

        @pl.when(l + 1 < layers)
        def _():
            for c in qkv_loads(l + 1):
                c.start()

        diag = jnp.where(col <= row, 0.0, -8e30).astype(F32)

        def block(i):
            lo, hi = i * QB, (i + 1) * QB
            for gr in range(heads // 2):
                pair_v = v_s[0:hi, gr * PAD:(gr + 1) * PAD]
                zero = jnp.zeros_like(pair_v)
                out = None
                for b in range(2):
                    h = 2 * gr + b
                    q = qk_s[lo:hi, h * PAD:(h + 1) * PAD]
                    kk = qk_s[0:hi, (heads + h) * PAD:(heads + h + 1) * PAD]
                    s = lax.dot_general(q, kk, (((1,), (1,)), ((), ())), preferred_element_type=F32)
                    sd = s[:, lo:] + diag
                    s = jnp.concatenate([s[:, :lo], sd], axis=1) if i else sd
                    m = jnp.max(s, axis=1, keepdims=True)
                    e = jnp.exp2((s - m) * scale)
                    total = jnp.sum(e, axis=1, keepdims=True)
                    pr = (e * (1.0 / total)).astype(BF16)
                    v = jnp.where(low, pair_v, zero) if b == 0 else jnp.where(low, zero, pair_v)
                    o = jnp.dot(pr, v, preferred_element_type=F32)
                    out = o if out is None else out + o
                heads_s[i, :, gr * PAD:(gr + 1) * PAD] = out.astype(BF16)

        def to_owner(i):
            return copy(heads_s.at[i], got.at[me], a_ss.at[i], a_rs.at[me], {"tp": me * 0 + i})

        for i in range(n):
            block(i)

            @pl.when(me != i)
            def _():
                to_owner(i).start()

            if i == n - 6:
                gw.near(0)
            elif i == n - 5:
                gw.near(1)
            elif i == n - 4:
                gw.near(2)
            elif i == n - 3:
                gw.near(3)
                gw.near(4)
            elif i == n - 2:
                gw.twin_near(0)
                gw.twin_near(1)
        for i in range(3):
            gw.far(i)
        gw.twin_near(2)
        gw.sibling()
        got[me] = heads_s[me]
        DN = 512

        def project(o, chip, core, first=False):
            a = got[2 * chip + core]

            def tile(j, _):
                cols = pl.ds(pl.multiple_of(j * DN, DN), DN)
                w = jnp.concatenate([big[slot(o, 0), core, :, cols], big[slot(o, 1), core, :, cols]], axis=0)
                y = jnp.dot(a, w, preferred_element_type=F32).astype(BF16).astype(F32)
                if first:
                    y = y + ob_ref[at_l, cols]
                res[:, cols] += y
                return 0

            lax.fori_loop(0, dm // DN, tile, 0)

        def arrive(src):
            copy(got.at[src], got.at[src], a_ss.at[src], a_rs.at[src], p.sib).wait_recv()

        arrive(2 * p.chip + 1 - k)
        project(OWN, p.chip, 0, True)
        project(OWN, p.chip, 1)
        gw.far(3)
        gw.far(4)
        gw.near_sibling()
        for o, chip in ((LEFT, p.left), (RIGHT, p.right)):
            for kk in range(2):
                arrive(2 * chip + kk)
                project(o, chip, kk)
        for i in range(3):
            gw.twin_far(i)
        gw.far_sibling()
        for kk in range(2):
            arrive(2 * p.opp + kk)
            project(OPP, p.opp, kk)
        gw.drain()
        for i in range(n):
            @pl.when(me != i)
            def _():
                to_owner(i).wait_send()

        norm_rows(n2g[at_l, :], n2s[at_l, :])
        gm = Gather(p, buf, mg_ss, mg_rs)
        cp = Copies(p)
        for c in range(4):
            gm.start(c)
        for c in mlp_loads(l):
            c.wait()
        UN, DN = 512, 512

        def feed(i):
            def up(j, _):
                cols = pl.ds(pl.multiple_of(j * UN, UN), UN)
                a = jnp.dot(buf[i].reshape(rows, dm), w_up[:, cols], preferred_element_type=F32) + ub_ref[at_l, cols]
                cdf = 0.5 * (1.0 + jnp.tanh(0.7978845608028654 * (a + 0.044715 * (a * a * a))))
                hid[:, cols] = (a * cdf).astype(BF16)
                return 0

            def down(j, _):
                cols = pl.ds(pl.multiple_of(j * DN, DN), DN)
                y = jnp.dot(hid[...], w_down[:, cols], preferred_element_type=F32).astype(BF16)
                big[i, :, :, cols] = y.reshape(2, HALF, DN)
                return 0

            lax.fori_loop(0, ff // UN, up, 0)
            lax.fori_loop(0, dm // DN, down, 0)

        def send_direct(s):
            cp.send(lambda: copy(big.at[slot(RIGHT, s), 1], direct.at[k, s], d_ss.at[0, s], d_rs.at[k, s], p.to_right[1]))
            cp.send(lambda: copy(big.at[slot(LEFT, s), 0], direct.at[k, s], d_ss.at[1, s], d_rs.at[k, s], p.to_left[0]))

        def send_opposite(s):
            for j in range(2):
                r = pl.ds(j * CH, CH)
                cp.send(lambda j=j, r=r: copy(big.at[slot(OPP, s), 0, r, :], omid.at[0, k, r, :], o_ss.at[0, s, j], o_rs.at[0, k, j], p.to_right[s]))
                cp.send(lambda j=j, r=r: copy(big.at[slot(OPP, s), 1, r, :], omid.at[1, k, r, :], o_ss.at[1, s, j], o_rs.at[1, k, j], p.to_left[s]))

        def m_one():
            gm.near(1)
            for s in range(2):
                cp.send(lambda s=s: copy(big.at[s, 1 - k], sibp.at[s], s_ss.at[s], s_rs.at[s], p.sib))

        def m_three():
            gm.near(2)
            gm.near(3)
            send_direct(0)

        def m_five():
            send_direct(1)
            cp.send(lambda: copy(big.at[3 + 2 * (1 - k), 0], midr.at[0], m_ss.at[0], m_rs.at[0], p.sib))
            cp.send(lambda: copy(big.at[2 + 2 * (1 - k), 1], midr.at[1], m_ss.at[1], m_rs.at[1], p.sib))

        run_steps(feed, arrivals(gm), {0: lambda: gm.near(0), 1: m_one, 3: m_three, 5: m_five, 6: lambda: send_opposite(0), 7: lambda: send_opposite(1)})
        for e in range(2):
            cp.recv(midr.at[e], m_ss.at[e], m_rs.at[e])
        for j in range(2):
            r = pl.ds(j * CH, CH)
            for e in range(2):
                for q in range(2):
                    cp.recv(omid.at[e, q, r, :], o_ss.at[e, q, j], o_rs.at[e, q, j])
                own = big[(3 if e == 0 else 2) + 2 * k, e, r, :].astype(F32)
                msum[e, r, :] = (own + midr[e, r, :].astype(F32)) + (omid[e, 0, r, :].astype(F32) + omid[e, 1, r, :].astype(F32))
                cp.send(lambda e=e, j=j, r=r: copy(msum.at[e, r, :], fin.at[k, r, :], f_ss.at[e, j], f_rs.at[k, j], p.to_right[0] if e == 0 else p.to_left[1]))
        for s in range(2):
            cp.recv(sibp.at[s], s_ss.at[s], s_rs.at[s])
            for q in range(2):
                cp.recv(direct.at[q, s], d_ss.at[q, s], d_rs.at[q, s])
            o = pl.ds(s * HALF, HALF)
            near = (big[s, k].astype(F32) + sibp[s].astype(F32)) + (direct[0, s].astype(F32) + direct[1, s].astype(F32))
            res[o, :] += near + db_ref[at_l, :]
        for j in range(2):
            r = pl.ds(j * CH, CH)
            for s in range(2):
                cp.recv(fin.at[s, r, :], f_ss.at[s, j], f_rs.at[s, j])
                o = pl.ds(s * HALF + j * CH, CH)
                res[o, :] += fin[s, r, :]
        gm.drain()
        cp.drain()

        @pl.when(l + 1 < layers)
        def _():
            p.greet(turn)

        return 0

    lax.fori_loop(0, layers, layer, 0)
    for d in range(1, n):
        copy(hot_ref, hots.at[me], h_ss.at[d - 1], h_rs.at[d - 1], {"tp": lax.rem(me + d, n)}).wait_send()

    def narrow(c, _):
        r = pl.ds(pl.multiple_of(c * CH, CH), CH)
        out_ref[r, :] = res[r, :].astype(BF16)
        return 0

    lax.fori_loop(0, 4, narrow, 0)


def solution(mesh):
    n = mesh.shape["tp"]
    row_spec = P("dp", "tp", None)
    vec_spec = P(None, None)
    in_specs = (row_spec, P("dp", "tp"), vec_spec, vec_spec, P(None, None, None, "tp", None), P(None, "tp", None, None), vec_spec, vec_spec, vec_spec, P(None, None, "tp"), P(None, "tp"), P(None, "tp", None), vec_spec)

    def device_fn(tokens, doc_ids, norm1_gain, norm1_shift, qkv_weight, out_weight, out_bias, norm2_gain, norm2_shift, up_weight, up_bias, down_weight, down_bias):
        layers, dm, _, heads, dim = qkv_weight.shape
        rows = tokens.shape[1]
        seq = n * rows
        ff = up_weight.shape[2]
        hot = (jnp.arange(16, dtype=jnp.int32)[:, None] == doc_ids).astype(BF16)
        qkv_t = jnp.transpose(qkv_weight, (0, 2, 3, 4, 1))
        out_w = out_weight.reshape(layers, heads * dim, dm)

        def body(*refs):
            kernel(n, *refs)

        vm = pl.BlockSpec(memory_space=pltpu.VMEM)
        hb = pl.BlockSpec(memory_space=pl.ANY)
        dma = pltpu.SemaphoreType.DMA
        v = pltpu.VMEM
        out = pl.pallas_call(
            body,
            out_shape=jax.ShapeDtypeStruct((rows, dm), BF16),
            in_specs=[vm, vm, vm, vm, hb, hb, vm, vm, vm, hb, vm, hb, vm],
            out_specs=vm,
            scratch_shapes=[
                v((rows, dm), F32),
                v((8, 2, HALF, dm), BF16),
                v((8, 2, HALF, dm), BF16),
                v((2 * heads, PAD, dm), BF16),
                v((heads * dim, dm), BF16),
                v((dm, ff), BF16),
                v((ff, dm), BF16),
                v((seq, 2 * heads * PAD), BF16),
                v((seq, heads * dim), BF16),
                v((seq, PAD), BF16),
                v((seq, PAD), BF16),
                v((n,) + hot.shape, BF16),
                v((n, rows, heads * dim), BF16),
                v((n, rows, heads * dim), BF16),
                v((rows, ff), BF16),
                v((2, HALF, dm), BF16),
                v((2, 2, HALF, dm), BF16),
                v((2, HALF, dm), BF16),
                v((2, 2, HALF, dm), BF16),
                v((2, HALF, dm), F32),
                v((2, HALF, dm), F32),
                dma((3 * heads + 4,)), pltpu.SemaphoreType.REGULAR,
                dma((n - 1,)), dma((n - 1,)), dma((7, 4)), dma((7, 4)), dma((10, 8)), dma((10, 8)), dma((7, 4)), dma((7, 4)), dma((n,)), dma((n,)),
                dma((2, 2)), dma((2, 2)), dma((2,)), dma((2,)), dma((2,)), dma((2,)),
                dma((2, 2, 2)), dma((2, 2, 2)), dma((2, 2)), dma((2, 2)),
            ],
            name="gpt_layers",
            compiler_params=pltpu.CompilerParams(collective_id=3, has_side_effects=True, vmem_limit_bytes=67_043_328),
        )(tokens[0], hot, norm1_gain, norm1_shift, qkv_t, out_w, out_bias, norm2_gain, norm2_shift, up_weight, up_bias, down_weight, down_bias)
        return out[None]

    return jax.shard_map(device_fn, mesh=mesh, in_specs=in_specs, out_specs=row_spec, check_vma=False)
```

time: 856 us -> 387 us (0.45); the launches traced: 847 us -> 387 us
  Pallas kernels: 0 us -> 384 us
  waiting for transfers between devices: 353 us -> 0 us
  blocking collectives: 207 us -> 0 us
  matrix products: 176 us -> 0 us
  other arithmetic: 67.5 us -> 1.28 us
  local copies, waits for them, and re-layouts: 18.9 us -> 2.3 us
  between operations: 14 us -> 0.01 us
  starting transfers between devices: 10.6 us -> 0 us
    pallas_call x0 -> x1, Pallas kernels: none -> 384 us  [device_fn(): pl.pallas_call(body, out_shape=jax.ShapeDtypeStruct((rows, dm), BF16), in...]
    all_to_all x2 -> x0, blocking collectives: 195 us -> none  [scatter_sum(): received = lax.all_to_all(split_rows, 'tp', 1, 1, tiled=True)]
    all_to_all x2 -> x0, waiting for transfers between devices: 185 us -> none  [scatter_sum(): received = lax.all_to_all(split_rows, 'tp', 1, 1, tiled=True)]
    all_gather x4 -> x0, waiting for transfers between devices: 168 us -> none  [the longest x2 92.9 us: device_fn(): full_rows2 = lax.all_gather(normed2, 'tp', axis=1, tiled=True)]
    dot_general x14 -> x0, matrix products: 111 us -> none  [the longest x2 51 us: device_fn(): jnp.einsum('bsf,fd->bsd', hidden, down_weight[layer_idx], preferred_eleme...]
    sub x6 -> x0, matrix products: 46.2 us -> none  [doc_causal_attention(): probs_blk = jax.nn.softmax(scores, axis=-1).astype(jnp.bfloat16)]
    sub x2 -> x0, other arithmetic: 32.8 us -> none  [doc_causal_attention(): probs_blk = jax.nn.softmax(scores, axis=-1).astype(jnp.bfloat16)]
    reduce_sum x12 -> x0, other arithmetic: 20 us -> none  [the longest x4 14.3 us: scatter_sum(): return jnp.sum(received, axis=1, dtype=jnp.float32)]
  transfers between devices with their start and end apart: 6 -> 0, of which waited for: 6 -> 0; matrix products, arithmetic and copies ran while one was open for 2% -> 0% of each run, Pallas kernels for 0% -> 0%
where the time goes in v4:
time: 387 us
  Pallas kernels  384 us (99%)
    pallas_call x1, Pallas kernels, device_fn(): pl.pallas_call(body, out_shape=jax.ShapeDtypeStruct((rows, dm), BF16), in...  384 us

profile of v4, /device:TPU:81, one launch (start us, length us, event | category | flops | bytes accessed | tf_op | source)
XLA Modules:
  0.0 387.3 jit_solution(1792250975322103287)
XLA Ops:
  0.0 1.3 fusion.refs_1_
  1.3 383.7 %gpt_layers.1 = bf16[256,2048]{1,0:T(8,128)(2,1)} custom-call(bf16[256,2048]{1,0:T(8,128)(2,1)} %bitcast.8, bf16[16,256]{1,0:T(8,128)(2,1)} %fusion.refs_1_, f32[2,2048]{1,0:T(2,128)} %refs_2_.1, f32[2,2048]{1,0:T(2,128)} %refs_3_.1, bf16[2,3,4,64,2048]{4,3,2,1,0:T(8,128)(2,1)} %bitcast.5, bf16[2,256,2048]{2,1,0:T(8,128)(2,1)} %bitcast.7, ...), custom_call_target="tpu_custom_call" | custom-call | tf_op jit(solution)/shard_map/gpt_layers/pallas_call | solution.py:601
  385.0 2.3 copy.15
